TPU v7x, 128 devices: a whole 4x4x4 slice. The times are simulated.
128 devices in a mesh: data: 1, group: 128 (over z, y, x, core).
Axes of the slice: x: 4, y: 4, z: 4, core: 2. Of those that a mesh axis runs over, the one named last changes fastest.
Arguments:
- latents: bfloat16 [2048, 768], P(('data', 'group'))
- hint_embed: bfloat16 [2048, 768], P(('data', 'group'))
- in_qkv: bfloat16 [2, 9, 768, 2304], replicated
- in_proj: bfloat16 [2, 9, 12, 64, 768], replicated
- in_up: bfloat16 [2, 9, 768, 3072], replicated
- in_down: bfloat16 [2, 9, 3072, 768], replicated
- in_norm: bfloat16 [2, 9, 4, 768], replicated
- out_qkv: bfloat16 [8, 768, 2304], replicated
- out_proj: bfloat16 [8, 12, 64, 768], replicated
- out_up: bfloat16 [8, 768, 3072], replicated
- out_down: bfloat16 [8, 3072, 768], replicated
- out_norm: bfloat16 [8, 4, 768], replicated
- zero_proj: bfloat16 [9, 768, 768], replicated
- hint_proj: bfloat16 [768, 768], replicated
- skip_proj: bfloat16 [8, 1536, 768], replicated
- final_norm: bfloat16 [2, 768], replicated
- w_out: bfloat16 [768, 768], replicated
Outputs:
- output: bfloat16 [2048, 768], P(('data', 'group'))
All inputs are finite; a program needn't handle non-finite values.
Results may differ from a plain program's by a relative error of at most 0.02.
Values are sent between devices in bfloat16 or wider.
A program may use at most 1.5 GiB of HBM per device.

v0:
```python
import jax
import jax.numpy as jnp
from jax import lax
from jax.sharding import PartitionSpec as P

EPS = 1e-6


def mat_f32(left_op, right_op):
    return jnp.dot(left_op, right_op, preferred_element_type=jnp.float32)


def layer_norm(values, norm_gain, norm_shift):
    wide_vals = values.astype(jnp.float32)
    centered = wide_vals - jnp.mean(wide_vals, axis=-1, keepdims=True)
    variance = jnp.mean(centered * centered, axis=-1, keepdims=True)
    normed = centered * lax.rsqrt(variance + EPS)
    return (normed * norm_gain.astype(jnp.float32) + norm_shift.astype(jnp.float32)).astype(jnp.bfloat16)


def gather_half(local_rows, half_size):
    gathered = local_rows
    offset_bit = 1
    while offset_bit < half_size:
        partner_perm = [(dev_id, dev_id ^ offset_bit) for dev_id in range(2 * half_size)]
        gathered = jnp.concatenate([gathered, lax.ppermute(gathered, "group", partner_perm)], axis=0)
        offset_bit = offset_bit * 2
    return gathered


def transformer_block(residual, w_qkv, w_proj, w_up, w_down, norm_rows, half_size):
    tok_count, model_width = residual.shape
    head_count, head_dim = w_proj.shape[0], w_proj.shape[1]
    normed = layer_norm(residual, norm_rows[0], norm_rows[1])
    qkv_all = mat_f32(normed, w_qkv).astype(jnp.bfloat16)
    queries = qkv_all[:, :model_width].reshape(tok_count, head_count, head_dim)
    key_vals = gather_half(qkv_all[:, model_width:], half_size)
    key_heads = key_vals[:, :model_width].reshape(-1, head_count, head_dim)
    val_heads = key_vals[:, model_width:].reshape(-1, head_count, head_dim)
    scores = jnp.einsum("thd,nhd->htn", queries, key_heads, preferred_element_type=jnp.float32) * head_dim ** -0.5
    att_probs = jax.nn.softmax(scores, axis=-1).astype(jnp.bfloat16)
    head_out = jnp.einsum("htn,nhd->thd", att_probs, val_heads, preferred_element_type=jnp.float32).astype(jnp.bfloat16)
    attn_sum = jnp.einsum("thd,hde->te", head_out, w_proj, preferred_element_type=jnp.float32)
    residual = (residual.astype(jnp.float32) + attn_sum).astype(jnp.bfloat16)
    normed = layer_norm(residual, norm_rows[2], norm_rows[3])
    hidden = jax.nn.gelu(mat_f32(normed, w_up), approximate=True).astype(jnp.bfloat16)
    return (residual.astype(jnp.float32) + mat_f32(hidden, w_down)).astype(jnp.bfloat16)


def solution(mesh):
    group_size = mesh.shape["group"]
    half_size = group_size // 2
    swap_perm = [(dev_id, (dev_id + half_size) % group_size) for dev_id in range(group_size)]
    to_base = [(dev_id + half_size, dev_id) for dev_id in range(half_size)]
    to_ctrl = [(dev_id, dev_id + half_size) for dev_id in range(half_size)]

    def device_step(x_own, hint_own, in_qkv, in_proj, in_up, in_down, in_norm, out_qkv, out_proj, out_up, out_down, out_norm, zero_proj, hint_proj, skip_proj, final_norm, w_out):
        layers = skip_proj.shape[0]
        tok_own, model_width = x_own.shape
        branch = lax.axis_index("group") // half_size
        is_base = branch == 0
        x_other = lax.ppermute(x_own, "group", swap_perm)
        hint_recv = lax.ppermute(hint_own, "group", to_ctrl)
        x_local = jnp.where(is_base, jnp.concatenate([x_own, x_other], axis=0), jnp.concatenate([x_other, x_own], axis=0))
        hint_local = jnp.where(is_base, jnp.zeros((2 * tok_own, model_width), jnp.bfloat16), jnp.concatenate([hint_recv, hint_own], axis=0))
        residual = (x_local.astype(jnp.float32) + mat_f32(hint_local, hint_proj)).astype(jnp.bfloat16)
        sum_list = []
        for layer_idx in range(layers + 1):
            residual = transformer_block(residual, in_qkv[branch, layer_idx], in_proj[branch, layer_idx], in_up[branch, layer_idx], in_down[branch, layer_idx], in_norm[branch, layer_idx], half_size)
            ctrl_res = mat_f32(residual, zero_proj[layer_idx]).astype(jnp.bfloat16)
            res_recv = lax.ppermute(ctrl_res, "group", to_base)
            sum_list.append((residual.astype(jnp.float32) + res_recv.astype(jnp.float32)).astype(jnp.bfloat16))
        out_state = sum_list.pop()
        for layer_idx in range(layers):
            skip_val = sum_list[layers - 1 - layer_idx]
            top_part = mat_f32(out_state, skip_proj[layer_idx, :model_width])
            low_part = mat_f32(skip_val, skip_proj[layer_idx, model_width:])
            merged = (top_part + low_part).astype(jnp.bfloat16)
            out_state = transformer_block(merged, out_qkv[layer_idx], out_proj[layer_idx], out_up[layer_idx], out_down[layer_idx], out_norm[layer_idx], half_size)
        normed = layer_norm(out_state, final_norm[0], final_norm[1])
        y_local = mat_f32(normed, w_out).astype(jnp.bfloat16)
        y_recv = lax.ppermute(y_local[tok_own:], "group", to_ctrl)
        return jnp.where(is_base, y_local[:tok_own], y_recv)

    tok_spec = P(("data", "group"), None)
    return jax.shard_map(device_step, mesh=mesh, in_specs=(tok_spec, tok_spec) + (P(),) * 15, out_specs=tok_spec, check_vma=False)
```

profile of v0, /device:TPU:1, one launch (start us, length us, event | category | flops | bytes accessed | tf_op | source)
XLA Modules:
  0.0 3016.7 jit_solution(7195515981997676401)
XLA Ops:
  57.4 31.3 %collective-permute-done.6 = bf16[512,1536]{1,0:T(8,128)(2,1)S(1)} collective-permute-done((bf16[512,1536]{1,0:T(8,128)(2,1)}, bf16[512,1536]{1,0:T(8,128)(2,1)S(1)}, u32[]{:S(2)}, u32[]{:S(2)}) %collective-permute-start.6) | collective-permute-done | bytes 1572896 | tf_op jit(solution)/shard_map/ppermute | solution.py:26
  91.6 64.5 %collective-permute-done.7 = bf16[1024,1536]{1,0:T(8,128)(2,1)S(1)} collective-permute-done((bf16[1024,1536]{1,0:T(8,128)(2,1)}, bf16[1024,1536]{1,0:T(8,128)(2,1)S(1)}, u32[]{:S(2)}, u32[]{:S(2)}) %collective-permute-start.7) | collective-permute-done | bytes 3145760 | tf_op jit(solution)/shard_map/ppermute | solution.py:26
  231.9 31.3 %collective-permute-done.12 = bf16[512,1536]{1,0:T(8,128)(2,1)S(1)} collective-permute-done((bf16[512,1536]{1,0:T(8,128)(2,1)}, bf16[512,1536]{1,0:T(8,128)(2,1)S(1)}, u32[]{:S(2)}, u32[]{:S(2)}) %collective-permute-start.12) | collective-permute-done | bytes 1572896 | tf_op jit(solution)/shard_map/ppermute | solution.py:26
  266.3 64.5 %collective-permute-done.13 = bf16[1024,1536]{1,0:T(8,128)(2,1)S(1)} collective-permute-done((bf16[1024,1536]{1,0:T(8,128)(2,1)}, bf16[1024,1536]{1,0:T(8,128)(2,1)S(1)}, u32[]{:S(2)}, u32[]{:S(2)}) %collective-permute-start.13) | collective-permute-done | bytes 3145760 | tf_op jit(solution)/shard_map/ppermute | solution.py:26
  406.6 31.3 %collective-permute-done.18 = bf16[512,1536]{1,0:T(8,128)(2,1)S(1)} collective-permute-done((bf16[512,1536]{1,0:T(8,128)(2,1)}, bf16[512,1536]{1,0:T(8,128)(2,1)S(1)}, u32[]{:S(2)}, u32[]{:S(2)}) %collective-permute-start.18) | collective-permute-done | bytes 1572896 | tf_op jit(solution)/shard_map/ppermute | solution.py:26
  440.9 64.5 %collective-permute-done.19 = bf16[1024,1536]{1,0:T(8,128)(2,1)S(1)} collective-permute-done((bf16[1024,1536]{1,0:T(8,128)(2,1)}, bf16[1024,1536]{1,0:T(8,128)(2,1)S(1)}, u32[]{:S(2)}, u32[]{:S(2)}) %collective-permute-start.19) | collective-permute-done | bytes 3145760 | tf_op jit(solution)/shard_map/ppermute | solution.py:26
  581.2 31.3 %collective-permute-done.24 = bf16[512,1536]{1,0:T(8,128)(2,1)S(1)} collective-permute-done((bf16[512,1536]{1,0:T(8,128)(2,1)}, bf16[512,1536]{1,0:T(8,128)(2,1)S(1)}, u32[]{:S(2)}, u32[]{:S(2)}) %collective-permute-start.24) | collective-permute-done | bytes 1572896 | tf_op jit(solution)/shard_map/ppermute | solution.py:26
  615.7 64.4 %collective-permute-done.25 = bf16[1024,1536]{1,0:T(8,128)(2,1)S(1)} collective-permute-done((bf16[1024,1536]{1,0:T(8,128)(2,1)}, bf16[1024,1536]{1,0:T(8,128)(2,1)S(1)}, u32[]{:S(2)}, u32[]{:S(2)}) %collective-permute-start.25) | collective-permute-done | bytes 3145760 | tf_op jit(solution)/shard_map/ppermute | solution.py:26
  756.0 31.3 %collective-permute-done.30 = bf16[512,1536]{1,0:T(8,128)(2,1)S(1)} collective-permute-done((bf16[512,1536]{1,0:T(8,128)(2,1)}, bf16[512,1536]{1,0:T(8,128)(2,1)S(1)}, u32[]{:S(2)}, u32[]{:S(2)}) %collective-permute-start.30) | collective-permute-done | bytes 1572896 | tf_op jit(solution)/shard_map/ppermute | solution.py:26
  790.6 64.4 %collective-permute-done.31 = bf16[1024,1536]{1,0:T(8,128)(2,1)S(1)} collective-permute-done((bf16[1024,1536]{1,0:T(8,128)(2,1)}, bf16[1024,1536]{1,0:T(8,128)(2,1)S(1)}, u32[]{:S(2)}, u32[]{:S(2)}) %collective-permute-start.31) | collective-permute-done | bytes 3145760 | tf_op jit(solution)/shard_map/ppermute | solution.py:26
  930.9 31.3 %collective-permute-done.36 = bf16[512,1536]{1,0:T(8,128)(2,1)S(1)} collective-permute-done((bf16[512,1536]{1,0:T(8,128)(2,1)}, bf16[512,1536]{1,0:T(8,128)(2,1)S(1)}, u32[]{:S(2)}, u32[]{:S(2)}) %collective-permute-start.36) | collective-permute-done | bytes 1572896 | tf_op jit(solution)/shard_map/ppermute | solution.py:26
  965.2 64.4 %collective-permute-done.37 = bf16[1024,1536]{1,0:T(8,128)(2,1)S(1)} collective-permute-done((bf16[1024,1536]{1,0:T(8,128)(2,1)}, bf16[1024,1536]{1,0:T(8,128)(2,1)S(1)}, u32[]{:S(2)}, u32[]{:S(2)}) %collective-permute-start.37) | collective-permute-done | bytes 3145760 | tf_op jit(solution)/shard_map/ppermute | solution.py:26
  1105.5 31.3 %collective-permute-done.42 = bf16[512,1536]{1,0:T(8,128)(2,1)S(1)} collective-permute-done((bf16[512,1536]{1,0:T(8,128)(2,1)}, bf16[512,1536]{1,0:T(8,128)(2,1)S(1)}, u32[]{:S(2)}, u32[]{:S(2)}) %collective-permute-start.42) | collective-permute-done | bytes 1572896 | tf_op jit(solution)/shard_map/ppermute | solution.py:26
  1139.9 64.4 %collective-permute-done.43 = bf16[1024,1536]{1,0:T(8,128)(2,1)S(1)} collective-permute-done((bf16[1024,1536]{1,0:T(8,128)(2,1)}, bf16[1024,1536]{1,0:T(8,128)(2,1)S(1)}, u32[]{:S(2)}, u32[]{:S(2)}) %collective-permute-start.43) | collective-permute-done | bytes 3145760 | tf_op jit(solution)/shard_map/ppermute | solution.py:26
  1280.3 31.3 %collective-permute-done.48 = bf16[512,1536]{1,0:T(8,128)(2,1)S(1)} collective-permute-done((bf16[512,1536]{1,0:T(8,128)(2,1)}, bf16[512,1536]{1,0:T(8,128)(2,1)S(1)}, u32[]{:S(2)}, u32[]{:S(2)}) %collective-permute-start.48) | collective-permute-done | bytes 1572896 | tf_op jit(solution)/shard_map/ppermute | solution.py:26
  1314.7 64.4 %collective-permute-done.49 = bf16[1024,1536]{1,0:T(8,128)(2,1)S(1)} collective-permute-done((bf16[1024,1536]{1,0:T(8,128)(2,1)}, bf16[1024,1536]{1,0:T(8,128)(2,1)S(1)}, u32[]{:S(2)}, u32[]{:S(2)}) %collective-permute-start.49) | collective-permute-done | bytes 3145760 | tf_op jit(solution)/shard_map/ppermute | solution.py:26
  1455.0 31.3 %collective-permute-done.54 = bf16[512,1536]{1,0:T(8,128)(2,1)S(1)} collective-permute-done((bf16[512,1536]{1,0:T(8,128)(2,1)}, bf16[512,1536]{1,0:T(8,128)(2,1)S(1)}, u32[]{:S(2)}, u32[]{:S(2)}) %collective-permute-start.54) | collective-permute-done | bytes 1572896 | tf_op jit(solution)/shard_map/ppermute | solution.py:26
  1493.9 59.8 %collective-permute-done.55 = bf16[1024,1536]{1,0:T(8,128)(2,1)S(1)} collective-permute-done((bf16[1024,1536]{1,0:T(8,128)(2,1)}, bf16[1024,1536]{1,0:T(8,128)(2,1)S(1)}, u32[]{:S(2)}, u32[]{:S(2)}) %collective-permute-start.55) | collective-permute-done | bytes 3145760 | tf_op jit(solution)/shard_map/ppermute | solution.py:26
  1639.9 31.3 %collective-permute-done.62 = bf16[512,1536]{1,0:T(8,128)(2,1)S(1)} collective-permute-done((bf16[512,1536]{1,0:T(8,128)(2,1)S(1)}, bf16[512,1536]{1,0:T(8,128)(2,1)S(1)}, u32[]{:S(2)}, u32[]{:S(2)}) %collective-permute-start.62) | collective-permute-done | bytes 1572896 | tf_op jit(solution)/shard_map/ppermute | solution.py:26
  1679.2 59.4 %collective-permute-done.63 = bf16[1024,1536]{1,0:T(8,128)(2,1)S(1)} collective-permute-done((bf16[1024,1536]{1,0:T(8,128)(2,1)}, bf16[1024,1536]{1,0:T(8,128)(2,1)S(1)}, u32[]{:S(2)}, u32[]{:S(2)}) %collective-permute-start.63) | collective-permute-done | bytes 3145760 | tf_op jit(solution)/shard_map/ppermute | solution.py:26
  1817.5 31.3 %collective-permute-done.69 = bf16[512,1536]{1,0:T(8,128)(2,1)S(1)} collective-permute-done((bf16[512,1536]{1,0:T(8,128)(2,1)S(1)}, bf16[512,1536]{1,0:T(8,128)(2,1)S(1)}, u32[]{:S(2)}, u32[]{:S(2)}) %collective-permute-start.69) | collective-permute-done | bytes 1572896 | tf_op jit(solution)/shard_map/ppermute | solution.py:26
  1855.4 60.7 %collective-permute-done.70 = bf16[1024,1536]{1,0:T(8,128)(2,1)S(1)} collective-permute-done((bf16[1024,1536]{1,0:T(8,128)(2,1)}, bf16[1024,1536]{1,0:T(8,128)(2,1)S(1)}, u32[]{:S(2)}, u32[]{:S(2)}) %collective-permute-start.70) | collective-permute-done | bytes 3145760 | tf_op jit(solution)/shard_map/ppermute | solution.py:26
  1995.0 31.3 %collective-permute-done.76 = bf16[512,1536]{1,0:T(8,128)(2,1)S(1)} collective-permute-done((bf16[512,1536]{1,0:T(8,128)(2,1)S(1)}, bf16[512,1536]{1,0:T(8,128)(2,1)S(1)}, u32[]{:S(2)}, u32[]{:S(2)}) %collective-permute-start.76) | collective-permute-done | bytes 1572896 | tf_op jit(solution)/shard_map/ppermute | solution.py:26
  2033.7 60.0 %collective-permute-done.77 = bf16[1024,1536]{1,0:T(8,128)(2,1)S(1)} collective-permute-done((bf16[1024,1536]{1,0:T(8,128)(2,1)}, bf16[1024,1536]{1,0:T(8,128)(2,1)S(1)}, u32[]{:S(2)}, u32[]{:S(2)}) %collective-permute-start.77) | collective-permute-done | bytes 3145760 | tf_op jit(solution)/shard_map/ppermute | solution.py:26
  2172.5 31.3 %collective-permute-done.83 = bf16[512,1536]{1,0:T(8,128)(2,1)S(1)} collective-permute-done((bf16[512,1536]{1,0:T(8,128)(2,1)S(1)}, bf16[512,1536]{1,0:T(8,128)(2,1)S(1)}, u32[]{:S(2)}, u32[]{:S(2)}) %collective-permute-start.83) | collective-permute-done | bytes 1572896 | tf_op jit(solution)/shard_map/ppermute | solution.py:26
  2210.7 60.5 %collective-permute-done.84 = bf16[1024,1536]{1,0:T(8,128)(2,1)S(1)} collective-permute-done((bf16[1024,1536]{1,0:T(8,128)(2,1)}, bf16[1024,1536]{1,0:T(8,128)(2,1)S(1)}, u32[]{:S(2)}, u32[]{:S(2)}) %collective-permute-start.84) | collective-permute-done | bytes 3145760 | tf_op jit(solution)/shard_map/ppermute | solution.py:26
  2350.1 31.3 %collective-permute-done.90 = bf16[512,1536]{1,0:T(8,128)(2,1)S(1)} collective-permute-done((bf16[512,1536]{1,0:T(8,128)(2,1)S(1)}, bf16[512,1536]{1,0:T(8,128)(2,1)S(1)}, u32[]{:S(2)}, u32[]{:S(2)}) %collective-permute-start.90) | collective-permute-done | bytes 1572896 | tf_op jit(solution)/shard_map/ppermute | solution.py:26
  2388.0 60.8 %collective-permute-done.91 = bf16[1024,1536]{1,0:T(8,128)(2,1)S(1)} collective-permute-done((bf16[1024,1536]{1,0:T(8,128)(2,1)}, bf16[1024,1536]{1,0:T(8,128)(2,1)S(1)}, u32[]{:S(2)}, u32[]{:S(2)}) %collective-permute-start.91) | collective-permute-done | bytes 3145760 | tf_op jit(solution)/shard_map/ppermute | solution.py:26
  2527.6 31.3 %collective-permute-done.97 = bf16[512,1536]{1,0:T(8,128)(2,1)S(1)} collective-permute-done((bf16[512,1536]{1,0:T(8,128)(2,1)S(1)}, bf16[512,1536]{1,0:T(8,128)(2,1)S(1)}, u32[]{:S(2)}, u32[]{:S(2)}) %collective-permute-start.97) | collective-permute-done | bytes 1572896 | tf_op jit(solution)/shard_map/ppermute | solution.py:26
  2565.5 60.7 %collective-permute-done.98 = bf16[1024,1536]{1,0:T(8,128)(2,1)S(1)} collective-permute-done((bf16[1024,1536]{1,0:T(8,128)(2,1)}, bf16[1024,1536]{1,0:T(8,128)(2,1)S(1)}, u32[]{:S(2)}, u32[]{:S(2)}) %collective-permute-start.98) | collective-permute-done | bytes 3145760 | tf_op jit(solution)/shard_map/ppermute | solution.py:26
  2743.1 60.7 %collective-permute-done.105 = bf16[1024,1536]{1,0:T(8,128)(2,1)S(1)} collective-permute-done((bf16[1024,1536]{1,0:T(8,128)(2,1)}, bf16[1024,1536]{1,0:T(8,128)(2,1)S(1)}, u32[]{:S(2)}, u32[]{:S(2)}) %collective-permute-start.105) | collective-permute-done | bytes 3145760 | tf_op jit(solution)/shard_map/ppermute | solution.py:26
  2917.1 64.4 %collective-permute-done.112 = bf16[1024,1536]{1,0:T(8,128)(2,1)S(1)} collective-permute-done((bf16[1024,1536]{1,0:T(8,128)(2,1)}, bf16[1024,1536]{1,0:T(8,128)(2,1)S(1)}, u32[]{:S(2)}, u32[]{:S(2)}) %collective-permute-start.112) | collective-permute-done | bytes 3145760 | tf_op jit(solution)/shard_map/ppermute | solution.py:26
  (758 shorter events, 1481.7 us)
Async XLA Ops:
  54.5 34.3 %collective-permute-start.6 = (bf16[512,1536]{1,0:T(8,128)(2,1)}, bf16[512,1536]{1,0:T(8,128)(2,1)S(1)}, u32[]{:S(2)}, u32[]{:S(2)}) collective-permute-start(bf16[512,1536]{1,0:T(8,128)(2,1)} %get-tuple-element.193), channel_id=1, source_target_pairs={{0,16},{1,17},{2,18},{3,19},{4,20},{5,21},{6,22},{7,23},{8,24},{9,... | collective-permute-start | bytes 4718600 | tf_op jit(solution)/shard_map/ppermute | solution.py:26
  90.7 65.4 %collective-permute-start.7 = (bf16[1024,1536]{1,0:T(8,128)(2,1)}, bf16[1024,1536]{1,0:T(8,128)(2,1)S(1)}, u32[]{:S(2)}, u32[]{:S(2)}) collective-permute-start(bf16[1024,1536]{1,0:T(8,128)(2,1)} %get-tuple-element.141), channel_id=1, source_target_pairs={{0,32},{1,33},{2,34},{3,35},{4,36},{5,37},{6,38},{7,39},{8,40},{9,... | collective-permute-start | bytes 9437192 | tf_op jit(solution)/shard_map/ppermute | solution.py:26
  229.0 34.3 %collective-permute-start.12 = (bf16[512,1536]{1,0:T(8,128)(2,1)}, bf16[512,1536]{1,0:T(8,128)(2,1)S(1)}, u32[]{:S(2)}, u32[]{:S(2)}) collective-permute-start(bf16[512,1536]{1,0:T(8,128)(2,1)} %get-tuple-element.190), channel_id=1, source_target_pairs={{0,16},{1,17},{2,18},{3,19},{4,20},{5,21},{6,22},{7,23},{8,24},{9,... | collective-permute-start | bytes 4718600 | tf_op jit(solution)/shard_map/ppermute | solution.py:26
  265.2 65.5 %collective-permute-start.13 = (bf16[1024,1536]{1,0:T(8,128)(2,1)}, bf16[1024,1536]{1,0:T(8,128)(2,1)S(1)}, u32[]{:S(2)}, u32[]{:S(2)}) collective-permute-start(bf16[1024,1536]{1,0:T(8,128)(2,1)} %get-tuple-element.139), channel_id=1, source_target_pairs={{0,32},{1,33},{2,34},{3,35},{4,36},{5,37},{6,38},{7,39},{8,40},{9,... | collective-permute-start | bytes 9437192 | tf_op jit(solution)/shard_map/ppermute | solution.py:26
  403.7 34.3 %collective-permute-start.18 = (bf16[512,1536]{1,0:T(8,128)(2,1)}, bf16[512,1536]{1,0:T(8,128)(2,1)S(1)}, u32[]{:S(2)}, u32[]{:S(2)}) collective-permute-start(bf16[512,1536]{1,0:T(8,128)(2,1)} %get-tuple-element.187), channel_id=1, source_target_pairs={{0,16},{1,17},{2,18},{3,19},{4,20},{5,21},{6,22},{7,23},{8,24},{9,... | collective-permute-start | bytes 4718600 | tf_op jit(solution)/shard_map/ppermute | solution.py:26
  439.9 65.5 %collective-permute-start.19 = (bf16[1024,1536]{1,0:T(8,128)(2,1)}, bf16[1024,1536]{1,0:T(8,128)(2,1)S(1)}, u32[]{:S(2)}, u32[]{:S(2)}) collective-permute-start(bf16[1024,1536]{1,0:T(8,128)(2,1)} %get-tuple-element.137), channel_id=1, source_target_pairs={{0,32},{1,33},{2,34},{3,35},{4,36},{5,37},{6,38},{7,39},{8,40},{9,... | collective-permute-start | bytes 9437192 | tf_op jit(solution)/shard_map/ppermute | solution.py:26
  578.3 34.3 %collective-permute-start.24 = (bf16[512,1536]{1,0:T(8,128)(2,1)}, bf16[512,1536]{1,0:T(8,128)(2,1)S(1)}, u32[]{:S(2)}, u32[]{:S(2)}) collective-permute-start(bf16[512,1536]{1,0:T(8,128)(2,1)} %get-tuple-element.184), channel_id=1, source_target_pairs={{0,16},{1,17},{2,18},{3,19},{4,20},{5,21},{6,22},{7,23},{8,24},{9,... | collective-permute-start | bytes 4718600 | tf_op jit(solution)/shard_map/ppermute | solution.py:26
  614.5 65.6 %collective-permute-start.25 = (bf16[1024,1536]{1,0:T(8,128)(2,1)}, bf16[1024,1536]{1,0:T(8,128)(2,1)S(1)}, u32[]{:S(2)}, u32[]{:S(2)}) collective-permute-start(bf16[1024,1536]{1,0:T(8,128)(2,1)} %get-tuple-element.135), channel_id=1, source_target_pairs={{0,32},{1,33},{2,34},{3,35},{4,36},{5,37},{6,38},{7,39},{8,40},{9,... | collective-permute-start | bytes 9437192 | tf_op jit(solution)/shard_map/ppermute | solution.py:26
  753.1 34.3 %collective-permute-start.30 = (bf16[512,1536]{1,0:T(8,128)(2,1)}, bf16[512,1536]{1,0:T(8,128)(2,1)S(1)}, u32[]{:S(2)}, u32[]{:S(2)}) collective-permute-start(bf16[512,1536]{1,0:T(8,128)(2,1)} %get-tuple-element.181), channel_id=1, source_target_pairs={{0,16},{1,17},{2,18},{3,19},{4,20},{5,21},{6,22},{7,23},{8,24},{9,... | collective-permute-start | bytes 4718600 | tf_op jit(solution)/shard_map/ppermute | solution.py:26
  789.3 65.8 %collective-permute-start.31 = (bf16[1024,1536]{1,0:T(8,128)(2,1)}, bf16[1024,1536]{1,0:T(8,128)(2,1)S(1)}, u32[]{:S(2)}, u32[]{:S(2)}) collective-permute-start(bf16[1024,1536]{1,0:T(8,128)(2,1)} %get-tuple-element.133), channel_id=1, source_target_pairs={{0,32},{1,33},{2,34},{3,35},{4,36},{5,37},{6,38},{7,39},{8,40},{9,... | collective-permute-start | bytes 9437192 | tf_op jit(solution)/shard_map/ppermute | solution.py:26
  928.0 34.3 %collective-permute-start.36 = (bf16[512,1536]{1,0:T(8,128)(2,1)}, bf16[512,1536]{1,0:T(8,128)(2,1)S(1)}, u32[]{:S(2)}, u32[]{:S(2)}) collective-permute-start(bf16[512,1536]{1,0:T(8,128)(2,1)} %get-tuple-element.178), channel_id=1, source_target_pairs={{0,16},{1,17},{2,18},{3,19},{4,20},{5,21},{6,22},{7,23},{8,24},{9,... | collective-permute-start | bytes 4718600 | tf_op jit(solution)/shard_map/ppermute | solution.py:26
  964.2 65.5 %collective-permute-start.37 = (bf16[1024,1536]{1,0:T(8,128)(2,1)}, bf16[1024,1536]{1,0:T(8,128)(2,1)S(1)}, u32[]{:S(2)}, u32[]{:S(2)}) collective-permute-start(bf16[1024,1536]{1,0:T(8,128)(2,1)} %get-tuple-element.131), channel_id=1, source_target_pairs={{0,32},{1,33},{2,34},{3,35},{4,36},{5,37},{6,38},{7,39},{8,40},{9,... | collective-permute-start | bytes 9437192 | tf_op jit(solution)/shard_map/ppermute | solution.py:26
  1138.8 65.5 %collective-permute-start.43 = (bf16[1024,1536]{1,0:T(8,128)(2,1)}, bf16[1024,1536]{1,0:T(8,128)(2,1)S(1)}, u32[]{:S(2)}, u32[]{:S(2)}) collective-permute-start(bf16[1024,1536]{1,0:T(8,128)(2,1)} %get-tuple-element.129), channel_id=1, source_target_pairs={{0,32},{1,33},{2,34},{3,35},{4,36},{5,37},{6,38},{7,39},{8,40},{9,... | collective-permute-start | bytes 9437192 | tf_op jit(solution)/shard_map/ppermute | solution.py:26
  1313.6 65.6 %collective-permute-start.49 = (bf16[1024,1536]{1,0:T(8,128)(2,1)}, bf16[1024,1536]{1,0:T(8,128)(2,1)S(1)}, u32[]{:S(2)}, u32[]{:S(2)}) collective-permute-start(bf16[1024,1536]{1,0:T(8,128)(2,1)} %get-tuple-element.127), channel_id=1, source_target_pairs={{0,32},{1,33},{2,34},{3,35},{4,36},{5,37},{6,38},{7,39},{8,40},{9,... | collective-permute-start | bytes 9437192 | tf_op jit(solution)/shard_map/ppermute | solution.py:26
  1488.3 65.4 %collective-permute-start.55 = (bf16[1024,1536]{1,0:T(8,128)(2,1)}, bf16[1024,1536]{1,0:T(8,128)(2,1)S(1)}, u32[]{:S(2)}, u32[]{:S(2)}) collective-permute-start(bf16[1024,1536]{1,0:T(8,128)(2,1)} %get-tuple-element.125), channel_id=1, source_target_pairs={{0,32},{1,33},{2,34},{3,35},{4,36},{5,37},{6,38},{7,39},{8,40},{9,... | collective-permute-start | bytes 9437192 | tf_op jit(solution)/shard_map/ppermute | solution.py:26
  1492.0 91.8 %collective-permute-start.57 = (bf16[32,768]{1,0:T(8,128)(2,1)}, bf16[32,768]{1,0:T(8,128)(2,1)}, u32[]{:S(2)}, u32[]{:S(2)}) collective-permute-start(bf16[32,768]{1,0:T(8,128)(2,1)} %fusion.816), channel_id=1, source_target_pairs={{64,0},{65,1},{66,2},{67,3},{68,4},{69,5},{70,6},{71,7},{72,8},{73... | collective-permute-start | bytes 147464 | tf_op jit(solution)/shard_map/ppermute | solution.py:71
  1673.2 65.4 %collective-permute-start.63 = (bf16[1024,1536]{1,0:T(8,128)(2,1)}, bf16[1024,1536]{1,0:T(8,128)(2,1)S(1)}, u32[]{:S(2)}, u32[]{:S(2)}) collective-permute-start(bf16[1024,1536]{1,0:T(8,128)(2,1)} %get-tuple-element.123), channel_id=1, source_target_pairs={{0,32},{1,33},{2,34},{3,35},{4,36},{5,37},{6,38},{7,39},{8,40},{9,... | collective-permute-start | bytes 9437192 | tf_op jit(solution)/shard_map/ppermute | solution.py:26
  1676.2 91.3 %collective-permute-start.64 = (bf16[32,768]{1,0:T(8,128)(2,1)}, bf16[32,768]{1,0:T(8,128)(2,1)}, u32[]{:S(2)}, u32[]{:S(2)}) collective-permute-start(bf16[32,768]{1,0:T(8,128)(2,1)} %fusion.819), channel_id=1, source_target_pairs={{64,0},{65,1},{66,2},{67,3},{68,4},{69,5},{70,6},{71,7},{72,8},{73... | collective-permute-start | bytes 147464 | tf_op jit(solution)/shard_map/ppermute | solution.py:71
  1850.8 65.4 %collective-permute-start.70 = (bf16[1024,1536]{1,0:T(8,128)(2,1)}, bf16[1024,1536]{1,0:T(8,128)(2,1)S(1)}, u32[]{:S(2)}, u32[]{:S(2)}) collective-permute-start(bf16[1024,1536]{1,0:T(8,128)(2,1)} %get-tuple-element.121), channel_id=1, source_target_pairs={{0,32},{1,33},{2,34},{3,35},{4,36},{5,37},{6,38},{7,39},{8,40},{9,... | collective-permute-start | bytes 9437192 | tf_op jit(solution)/shard_map/ppermute | solution.py:26
  1853.7 91.3 %collective-permute-start.71 = (bf16[32,768]{1,0:T(8,128)(2,1)}, bf16[32,768]{1,0:T(8,128)(2,1)}, u32[]{:S(2)}, u32[]{:S(2)}) collective-permute-start(bf16[32,768]{1,0:T(8,128)(2,1)} %fusion.822), channel_id=1, source_target_pairs={{64,0},{65,1},{66,2},{67,3},{68,4},{69,5},{70,6},{71,7},{72,8},{73... | collective-permute-start | bytes 147464 | tf_op jit(solution)/shard_map/ppermute | solution.py:71
  2028.3 65.4 %collective-permute-start.77 = (bf16[1024,1536]{1,0:T(8,128)(2,1)}, bf16[1024,1536]{1,0:T(8,128)(2,1)S(1)}, u32[]{:S(2)}, u32[]{:S(2)}) collective-permute-start(bf16[1024,1536]{1,0:T(8,128)(2,1)} %get-tuple-element.119), channel_id=1, source_target_pairs={{0,32},{1,33},{2,34},{3,35},{4,36},{5,37},{6,38},{7,39},{8,40},{9,... | collective-permute-start | bytes 9437192 | tf_op jit(solution)/shard_map/ppermute | solution.py:26
  2032.0 90.6 %collective-permute-start.78 = (bf16[32,768]{1,0:T(8,128)(2,1)}, bf16[32,768]{1,0:T(8,128)(2,1)S(1)}, u32[]{:S(2)}, u32[]{:S(2)}) collective-permute-start(bf16[32,768]{1,0:T(8,128)(2,1)} %fusion.825), channel_id=1, source_target_pairs={{64,0},{65,1},{66,2},{67,3},{68,4},{69,5},{70,6},{71,7},{72,8},{73... | collective-permute-start | bytes 147464 | tf_op jit(solution)/shard_map/ppermute | solution.py:71
  2205.8 65.4 %collective-permute-start.84 = (bf16[1024,1536]{1,0:T(8,128)(2,1)}, bf16[1024,1536]{1,0:T(8,128)(2,1)S(1)}, u32[]{:S(2)}, u32[]{:S(2)}) collective-permute-start(bf16[1024,1536]{1,0:T(8,128)(2,1)} %get-tuple-element.117), channel_id=1, source_target_pairs={{0,32},{1,33},{2,34},{3,35},{4,36},{5,37},{6,38},{7,39},{8,40},{9,... | collective-permute-start | bytes 9437192 | tf_op jit(solution)/shard_map/ppermute | solution.py:26
  2208.8 91.4 %collective-permute-start.85 = (bf16[32,768]{1,0:T(8,128)(2,1)}, bf16[32,768]{1,0:T(8,128)(2,1)S(1)}, u32[]{:S(2)}, u32[]{:S(2)}) collective-permute-start(bf16[32,768]{1,0:T(8,128)(2,1)} %fusion.828), channel_id=1, source_target_pairs={{64,0},{65,1},{66,2},{67,3},{68,4},{69,5},{70,6},{71,7},{72,8},{73... | collective-permute-start | bytes 147464 | tf_op jit(solution)/shard_map/ppermute | solution.py:71
  2347.2 34.3 %collective-permute-start.90 = (bf16[512,1536]{1,0:T(8,128)(2,1)S(1)}, bf16[512,1536]{1,0:T(8,128)(2,1)S(1)}, u32[]{:S(2)}, u32[]{:S(2)}) collective-permute-start(bf16[512,1536]{1,0:T(8,128)(2,1)S(1)} %get-tuple-element.154), channel_id=1, source_target_pairs={{0,16},{1,17},{2,18},{3,19},{4,20},{5,21},{6,22},{7,23},{8,24},{9,... | collective-permute-start | bytes 4718600 | tf_op jit(solution)/shard_map/ppermute | solution.py:26
  2383.4 65.4 %collective-permute-start.91 = (bf16[1024,1536]{1,0:T(8,128)(2,1)}, bf16[1024,1536]{1,0:T(8,128)(2,1)S(1)}, u32[]{:S(2)}, u32[]{:S(2)}) collective-permute-start(bf16[1024,1536]{1,0:T(8,128)(2,1)} %get-tuple-element.115), channel_id=1, source_target_pairs={{0,32},{1,33},{2,34},{3,35},{4,36},{5,37},{6,38},{7,39},{8,40},{9,... | collective-permute-start | bytes 9437192 | tf_op jit(solution)/shard_map/ppermute | solution.py:26
  2386.3 91.4 %collective-permute-start.92 = (bf16[32,768]{1,0:T(8,128)(2,1)}, bf16[32,768]{1,0:T(8,128)(2,1)S(1)}, u32[]{:S(2)}, u32[]{:S(2)}) collective-permute-start(bf16[32,768]{1,0:T(8,128)(2,1)} %fusion.831), channel_id=1, source_target_pairs={{64,0},{65,1},{66,2},{67,3},{68,4},{69,5},{70,6},{71,7},{72,8},{73... | collective-permute-start | bytes 147464 | tf_op jit(solution)/shard_map/ppermute | solution.py:71
  2560.9 65.4 %collective-permute-start.98 = (bf16[1024,1536]{1,0:T(8,128)(2,1)}, bf16[1024,1536]{1,0:T(8,128)(2,1)S(1)}, u32[]{:S(2)}, u32[]{:S(2)}) collective-permute-start(bf16[1024,1536]{1,0:T(8,128)(2,1)} %get-tuple-element.113), channel_id=1, source_target_pairs={{0,32},{1,33},{2,34},{3,35},{4,36},{5,37},{6,38},{7,39},{8,40},{9,... | collective-permute-start | bytes 9437192 | tf_op jit(solution)/shard_map/ppermute | solution.py:26
  2563.9 91.4 %collective-permute-start.99 = (bf16[32,768]{1,0:T(8,128)(2,1)}, bf16[32,768]{1,0:T(8,128)(2,1)S(1)}, u32[]{:S(2)}, u32[]{:S(2)}) collective-permute-start(bf16[32,768]{1,0:T(8,128)(2,1)} %fusion.834), channel_id=1, source_target_pairs={{64,0},{65,1},{66,2},{67,3},{68,4},{69,5},{70,6},{71,7},{72,8},{73... | collective-permute-start | bytes 147464 | tf_op jit(solution)/shard_map/ppermute | solution.py:71
  2738.4 65.4 %collective-permute-start.105 = (bf16[1024,1536]{1,0:T(8,128)(2,1)}, bf16[1024,1536]{1,0:T(8,128)(2,1)S(1)}, u32[]{:S(2)}, u32[]{:S(2)}) collective-permute-start(bf16[1024,1536]{1,0:T(8,128)(2,1)} %get-tuple-element.111), channel_id=1, source_target_pairs={{0,32},{1,33},{2,34},{3,35},{4,36},{5,37},{6,38},{7,39},{8,40},{9,... | collective-permute-start | bytes 9437192 | tf_op jit(solution)/shard_map/ppermute | solution.py:26
  2741.4 91.3 %collective-permute-start.106 = (bf16[32,768]{1,0:T(8,128)(2,1)}, bf16[32,768]{1,0:T(8,128)(2,1)S(1)}, u32[]{:S(2)}, u32[]{:S(2)}) collective-permute-start(bf16[32,768]{1,0:T(8,128)(2,1)} %fusion.837), channel_id=1, source_target_pairs={{64,0},{65,1},{66,2},{67,3},{68,4},{69,5},{70,6},{71,7},{72,8},{73... | collective-permute-start | bytes 147464 | tf_op jit(solution)/shard_map/ppermute | solution.py:71
  2915.9 65.6 %collective-permute-start.112 = (bf16[1024,1536]{1,0:T(8,128)(2,1)}, bf16[1024,1536]{1,0:T(8,128)(2,1)S(1)}, u32[]{:S(2)}, u32[]{:S(2)}) collective-permute-start(bf16[1024,1536]{1,0:T(8,128)(2,1)} %get-tuple-element.109), channel_id=1, source_target_pairs={{0,32},{1,33},{2,34},{3,35},{4,36},{5,37},{6,38},{7,39},{8,40},{9,... | collective-permute-start | bytes 9437192 | tf_op jit(solution)/shard_map/ppermute | solution.py:26
  (124 other events, 2141.8 us)
where the time goes:
time: 3030 us; the launch traced here: 3020 us
  waiting for transfers between devices  2060 us (68%)
  local copies, waits for them, and re-layouts  366 us (12%)
  matrix products  297 us (10%)
  starting transfers between devices  269 us (9%)
    ppermute x102, waiting for transfers between devices, gather_half(): lax.ppermute(gathered, 'group', partner_perm)  2050 us
    ppermute x102, starting transfers between devices, gather_half(): lax.ppermute(gathered, 'group', partner_perm)  243 us
    dot_general x61, matrix products, mat_f32(): return jnp.dot(left_op, right_op, preferred_element_type=jnp.float32)  191 us
    slice x34, local copies, waits for them, and re-layouts, transformer_block(): key_heads = key_vals[:, :model_width].reshape(-1, head_count, head_dim)  134 us
    slice x17, local copies, waits for them, and re-layouts, transformer_block(): val_heads = key_vals[:, model_width:].reshape(-1, head_count, head_dim)  80.9 us
    unnamed x169, local copies, waits for them, and re-layouts  80.9 us
    concatenate x34, local copies, waits for them, and re-layouts, gather_half(): jnp.concatenate([gathered, lax.ppermute(gathered, 'group', partner_perm)]...  65.6 us
    dot_general x17, matrix products, transformer_block(): jnp.einsum('thd,hde->te', head_out, w_proj, preferred_element_type=jnp.fl...  63.2 us
  transfers between devices with their start and end apart: 114, of which 105 were waited for; matrix products, arithmetic and copies ran while one was open for 10% of the time, Pallas kernels for 0%

commit v1 on v0

v1 whole, which is shorter than its diff:
```python
import functools

import jax
import jax.numpy as jnp
from jax import lax
from jax.experimental import pallas as pl
from jax.experimental.pallas import tpu as pltpu
from jax.sharding import PartitionSpec as P

EPS = 1e-6
MESH = pl.DeviceIdType.MESH
LOG2E = 1.4426950408889634
ROWS = 32
HALF_ROWS = 16


def mat_f32(left_op, right_op):
    return jnp.dot(left_op, right_op, preferred_element_type=jnp.float32)


def layer_norm(values, gain, shift):
    wide_vals = values.astype(jnp.float32)
    centered = wide_vals - jnp.mean(wide_vals, axis=-1, keepdims=True)
    variance = jnp.mean(centered * centered, axis=-1, keepdims=True)
    normed = centered * lax.rsqrt(variance + EPS)
    return (normed * gain.astype(jnp.float32) + shift.astype(jnp.float32)).astype(jnp.bfloat16)


def gelu(v):
    inner = 0.7978845608028654 * (v + 0.044715 * (v * v * v))
    return 0.5 * v * (1.0 + jnp.tanh(inner))


def stack_kernel(n_blocks, two_branch, has_skip, *refs):
    if has_skip:
        x_ref, s_ref, norm_ref, skip_hbm, qkv_hbm, proj_hbm, up_hbm, down_hbm, out_ref, *scratch = refs
        (w_skip, *scratch) = scratch
    else:
        x_ref, norm_ref, qkv_hbm, proj_hbm, up_hbm, down_hbm, out_ref, *scratch = refs
    (t_all, w_qkv, w_proj, w_up, w_down, v_buf, s_buf, m_buf, a_buf, a_full, u_buf,
     w_sem, p1, p2, p3, s1, s2, s3, a_recv, q1, q2, q3, f1, f2, f3, a_send) = scratch
    width = x_ref.shape[-1]
    half_w = width // 2
    hid = w_up.shape[-1]

    data_idx = lax.axis_index("data")
    me = lax.axis_index("group")
    core = lax.rem(me, 2)
    chip = me // 2
    x_pos = lax.rem(chip, 4)
    y_pos = lax.rem(chip // 4, 4)
    z_full = chip // 16
    half = z_full // 2
    z_pos = lax.rem(z_full, 2)
    sib_core = 1 - core
    sibling = me + 1 - 2 * core

    def dev(zz, yy, xx):
        return (((half * 2 + zz) * 4 + yy) * 4 + xx) * 2 + core

    def shift(pos, d):
        return lax.rem(pos + d + 4, 4)

    def z_of(dz):
        return z_pos if dz == 0 else 1 - z_pos

    relay = (y_pos, x_pos)

    def group(par, k, cc, zz, r):
        if k == 0:
            return t_all.at[par, cc, zz, r, :, pl.ds(0, HALF_ROWS), :]
        return t_all.at[par, cc, zz, :, r, pl.ds(HALF_ROWS, HALF_ROWS), :]

    def piece(par, k, zz, yy, xx):
        return t_all.at[par, core, zz, yy, xx, pl.ds(k * HALF_ROWS, HALF_ROWS), :]

    def remote(region, target, send_sem, recv_sem):
        return pltpu.make_async_remote_copy(
            src_ref=region, dst_ref=region, send_sem=send_sem, recv_sem=recv_sem,
            device_id=(data_idx, target), device_id_type=MESH)

    def leg1(par, k, dz, d, receive=False):
        sems = (q1.at[k, dz, d], p1.at[par, k, dz, d])
        if receive:
            src = (z_of(dz), y_pos, shift(x_pos, -d)) if k == 0 else (z_of(dz), shift(y_pos, -d), x_pos)
            return remote(piece(par, k, *src), dev(*src), *sems)
        dst = (z_of(dz), y_pos, shift(x_pos, d)) if k == 0 else (z_of(dz), shift(y_pos, d), x_pos)
        return remote(piece(par, k, z_pos, y_pos, x_pos), dev(*dst), *sems)

    def along(k, d):
        return dev(z_pos, shift(y_pos, d), x_pos) if k == 0 else dev(z_pos, y_pos, shift(x_pos, d))

    step_of = (1, -1)

    def leg2(par, k, dz, way, receive=False):
        sems = (q2.at[k, dz, way], p2.at[par, k, dz, way])
        d = step_of[way]
        at = shift(relay[k], -d) if receive else relay[k]
        return remote(group(par, k, core, z_of(dz), at), along(k, d), *sems)

    def leg3(par, k, way, receive=False):
        sems = (q3.at[k, way], p3.at[par, k, way])
        d = step_of[way]
        at = shift(relay[k], -2 * d) if receive else shift(relay[k], -d)
        return remote(group(par, k, core, z_of(way), at), along(k, d), *sems)

    def side1(par, k, dz, cc):
        return remote(group(par, k, cc, z_of(dz), relay[k]), sibling, f1.at[k, dz], s1.at[par, k, dz])

    def side2(par, k, dz, way, cc):
        region = group(par, k, cc, z_of(dz), shift(relay[k], -step_of[way]))
        return remote(region, sibling, f2.at[k, dz, way], s2.at[par, k, dz, way])

    def side3(par, k, way, cc):
        region = group(par, k, cc, z_of(way), shift(relay[k], 2))
        return remote(region, sibling, f3.at[k, way], s3.at[par, k, way])

    leg1_keys = [(k, dz, d) for dz, d in ((1, 2), (0, 2), (1, 1), (1, 3), (0, 1), (0, 3), (1, 0)) for k in (0, 1)]

    def layer_of(ref, i):
        return ref.at[half, i] if two_branch else ref.at[i]

    def qkv_copies(i):
        cols = lambda part: pl.ds(pl.multiple_of(part * width + core * half_w, 128), half_w)
        return [pltpu.make_async_copy(layer_of(qkv_hbm, i).at[:, cols(p)], w_qkv.at[:, pl.ds(p * half_w, half_w)], w_sem.at[p]) for p in range(3)]

    def proj_copies(i):
        return [pltpu.make_async_copy(layer_of(proj_hbm, i), w_proj, w_sem.at[3])]

    def up_copies(i):
        return [pltpu.make_async_copy(layer_of(up_hbm, i), w_up, w_sem.at[4])]

    def down_copies(i):
        return [pltpu.make_async_copy(layer_of(down_hbm, i), w_down, w_sem.at[5])]

    def skip_copies(i):
        return [pltpu.make_async_copy(skip_hbm.at[i], w_skip, w_sem.at[6])]

    def start(copies):
        for c in copies:
            c.start()

    def wait(copies):
        for c in copies:
            c.wait()

    def start_next(make, i):
        @pl.when(i + 1 < n_blocks)
        def _():
            start(make(i + 1))

    if has_skip:
        start(skip_copies(0))
    for make in (qkv_copies, proj_copies, up_copies, down_copies):
        start(make(0))
    u_buf[...] = x_ref[...]

    lane = lax.broadcasted_iota(jnp.int32, (2 * ROWS, 128), 1)

    def block(i, carry):
        par = lax.rem(i, 2)
        if has_skip:
            wait(skip_copies(i))
            merged = mat_f32(u_buf[...], w_skip[0:width, :]) + mat_f32(s_ref[i], w_skip[width:2 * width, :])
            u_buf[...] = merged.astype(jnp.bfloat16)
            start_next(skip_copies, i)
        t = layer_norm(u_buf[...], norm_ref[i, 0:1, :], norm_ref[i, 1:2, :])
        t_all[par, core, z_pos, y_pos, x_pos] = t
        for key in leg1_keys:
            leg1(par, *key).start()

        for dz in (0, 1):
            for k in (0, 1):
                for d in range(4):
                    if dz or d:
                        leg1(par, k, dz, d, receive=True).wait_recv()
                leg2(par, k, dz, 0).start()
                leg2(par, k, dz, 1).start()
                side1(par, k, dz, core).start()

        wait(qkv_copies(i))

        def chunk(j, k, r):
            rows = []
            for cc in range(2):
                for zz in range(2):
                    for o in range(4):
                        if k == 0:
                            rows.append(t_all[par, cc, zz, r, o, 0:HALF_ROWS, :])
                        else:
                            rows.append(t_all[par, cc, zz, o, r, HALF_ROWS:ROWS, :])
            toks = jnp.concatenate(rows, axis=0)
            n = toks.shape[0]
            kv = mat_f32(toks, w_qkv[:, half_w:3 * half_w]).astype(jnp.bfloat16)
            v_buf[j * n:(j + 1) * n, :] = kv[:, half_w:]
            for p in range(3):
                sc = lax.dot_general(q_bd[p], kv[:, p * 128:(p + 1) * 128], (((1,), (1,)), ((), ())), preferred_element_type=jnp.float32)
                s_buf[p, :, j * n:(j + 1) * n] = sc
                top = jnp.maximum(sc[:, 0:128], sc[:, 128:256])
                m_buf[p] = top if j == 0 else jnp.maximum(m_buf[p], top)

        for dz in (0, 1):
            for k in (0, 1):
                side1(par, k, dz, sib_core).wait_recv()
        own = jnp.concatenate([t_all[par, 0, z_pos, y_pos, x_pos], t_all[par, 1, z_pos, y_pos, x_pos]], axis=0)
        q = mat_f32(own, w_qkv[:, 0:half_w])
        q_bd = []
        for p in range(3):
            qp = q[:, p * 128:(p + 1) * 128]
            q_bd.append(jnp.concatenate([jnp.where(lane < 64, qp, 0.0), jnp.where(lane < 64, 0.0, qp)], axis=0).astype(jnp.bfloat16))

        chunk(0, 0, relay[0])

        def take2(k, dz, way, forward):
            leg2(par, k, dz, way, receive=True).wait_recv()
            if forward:
                leg3(par, k, way).start()
            side2(par, k, dz, way, core).start()

        take2(0, 0, 0, True)
        take2(1, 0, 0, True)
        chunk(1, 1, relay[1])
        take2(0, 1, 1, True)
        take2(1, 1, 1, True)
        for k in (0, 1):
            take2(k, 1, 0, False)
            take2(k, 0, 1, False)
        j = 2
        for k in (0, 1):
            for way in (0, 1):
                for dz in (0, 1):
                    side2(par, k, dz, way, sib_core).wait_recv()
                chunk(j, k, shift(relay[k], -step_of[way]))
                j += 1
        for k in (0, 1):
            for way in (0, 1):
                leg3(par, k, way, receive=True).wait_recv()
                side3(par, k, way, core).start()
        for k in (0, 1):
            for way in (0, 1):
                side3(par, k, way, sib_core).wait_recv()
            chunk(j, k, shift(relay[k], 2))
            j += 1
        start_next(qkv_copies, i)

        n_chunks, n = 8, 256
        scale = 64 ** -0.5 * LOG2E
        for p in range(3):
            top = jnp.max(m_buf[p], axis=-1, keepdims=True)
            part = None
            for j in range(n_chunks):
                e = jnp.exp2((s_buf[p, :, j * n:(j + 1) * n] - top) * scale)
                s_buf[p, :, j * n:(j + 1) * n] = e
                both = e[:, 0:128] + e[:, 128:256]
                part = both if part is None else part + both
            inv = 1.0 / jnp.sum(part, axis=-1, keepdims=True)
            acc = None
            for j in range(n_chunks):
                pr = (s_buf[p, :, j * n:(j + 1) * n] * inv).astype(jnp.bfloat16)
                o = mat_f32(pr, v_buf[j * n:(j + 1) * n, p * 128:(p + 1) * 128])
                acc = o if acc is None else acc + o
            a = jnp.where(lane < 64, acc[0:2 * ROWS], acc[2 * ROWS:4 * ROWS]).astype(jnp.bfloat16)
            a_buf[0, :, p * 128:(p + 1) * 128] = a[0:ROWS]
            a_buf[1, :, p * 128:(p + 1) * 128] = a[ROWS:2 * ROWS]

        swap = pltpu.make_async_remote_copy(
            src_ref=a_buf.at[sib_core], dst_ref=a_full.at[core], send_sem=a_send, recv_sem=a_recv,
            device_id=(data_idx, sibling), device_id_type=MESH)
        swap.start()
        a_full[core] = a_buf[core]
        swap.wait_send()
        pltpu.make_async_remote_copy(
            src_ref=a_buf.at[core], dst_ref=a_full.at[sib_core], send_sem=a_send, recv_sem=a_recv,
            device_id=(data_idx, sibling), device_id_type=MESH).wait_recv()

        wait(proj_copies(i))
        attn = mat_f32(a_full[0], w_proj[0:half_w, :]) + mat_f32(a_full[1], w_proj[half_w:width, :])
        start_next(proj_copies, i)
        mid = (u_buf[...].astype(jnp.float32) + attn).astype(jnp.bfloat16)
        t2 = layer_norm(mid, norm_ref[i, 2:3, :], norm_ref[i, 3:4, :])
        wait(up_copies(i))
        wait(down_copies(i))
        acc = None
        for c in range(0, hid, width):
            h = gelu(mat_f32(t2, w_up[:, c:c + width])).astype(jnp.bfloat16)
            o = mat_f32(h, w_down[c:c + width, :])
            acc = o if acc is None else acc + o
        start_next(up_copies, i)
        start_next(down_copies, i)
        res = (mid.astype(jnp.float32) + acc).astype(jnp.bfloat16)
        u_buf[...] = res
        if not has_skip:
            out_ref[i] = res

        for key in leg1_keys:
            leg1(par, *key).wait_send()
        for k in (0, 1):
            for way in (0, 1):
                for dz in (0, 1):
                    leg2(par, k, dz, way).wait_send()
                    side2(par, k, dz, way, core).wait_send()
                leg3(par, k, way).wait_send()
                side3(par, k, way, core).wait_send()
            for dz in (0, 1):
                side1(par, k, dz, core).wait_send()
        return carry

    lax.fori_loop(0, n_blocks, block, 0)
    if has_skip:
        out_ref[...] = u_buf[...]


def run_stack(x, norm, qkv, proj, up, down, skip=None, s=None):
    two_branch = qkv.ndim == 4
    has_skip = skip is not None
    n_blocks, width, hid = norm.shape[0], x.shape[-1], up.shape[-1]
    vmem, hbm = pl.BlockSpec(memory_space=pltpu.VMEM), pl.BlockSpec(memory_space=pl.ANY)
    bf, f32, dma = jnp.bfloat16, jnp.float32, pltpu.SemaphoreType.DMA
    scratch = [
        pltpu.VMEM((2, 2, 2, 4, 4, ROWS, width), bf),
        pltpu.VMEM((width, 3 * width // 2), bf),
        pltpu.VMEM((width, width), bf),
        pltpu.VMEM((width, hid), bf),
        pltpu.VMEM((hid, width), bf),
        pltpu.VMEM((2048, width // 2), bf),
        pltpu.VMEM((3, 128, 2048), f32),
        pltpu.VMEM((3, 128, 128), f32),
        pltpu.VMEM((2, ROWS, width // 2), bf),
        pltpu.VMEM((2, ROWS, width // 2), bf),
        pltpu.VMEM((ROWS, width), bf),
        dma((7,)),
        dma((2, 2, 2, 4)), dma((2, 2, 2, 2)), dma((2, 2, 2)),
        dma((2, 2, 2)), dma((2, 2, 2, 2)), dma((2, 2, 2)), dma(()),
        dma((2, 2, 4)), dma((2, 2, 2)), dma((2, 2)),
        dma((2, 2)), dma((2, 2, 2)), dma((2, 2)), dma(()),
    ]
    if has_skip:
        scratch = [pltpu.VMEM((2 * width, width), bf)] + scratch
        args, specs = (x, s, norm, skip, qkv, proj, up, down), [vmem] * 3 + [hbm] * 5
        out = jax.ShapeDtypeStruct((ROWS, width), bf)
    else:
        args, specs = (x, norm, qkv, proj, up, down), [vmem] * 2 + [hbm] * 4
        out = jax.ShapeDtypeStruct((n_blocks, ROWS, width), bf)
    return pl.pallas_call(
        functools.partial(stack_kernel, n_blocks, two_branch, has_skip),
        out_shape=out, in_specs=specs, out_specs=vmem, scratch_shapes=scratch,
        name="out_stack" if has_skip else "in_stack",
        compiler_params=pltpu.CompilerParams(has_side_effects=True, vmem_limit_bytes=48 * 1024 * 1024),
    )(*args)


def solution(mesh):
    group_size = mesh.shape["group"]
    half_size = group_size // 2
    swap_perm = [(dev_id, (dev_id + half_size) % group_size) for dev_id in range(group_size)]
    to_base = [(dev_id + half_size, dev_id) for dev_id in range(half_size)]
    to_ctrl = [(dev_id, dev_id + half_size) for dev_id in range(half_size)]

    def device_step(x_own, hint_own, in_qkv, in_proj, in_up, in_down, in_norm, out_qkv, out_proj, out_up, out_down, out_norm, zero_proj, hint_proj, skip_proj, final_norm, w_out):
        layers = skip_proj.shape[0]
        tok_own, model_width = x_own.shape
        branch = lax.axis_index("group") // half_size
        is_base = branch == 0
        x_other = lax.ppermute(x_own, "group", swap_perm)
        hint_recv = lax.ppermute(hint_own, "group", to_ctrl)
        x_local = jnp.where(is_base, jnp.concatenate([x_own, x_other], axis=0), jnp.concatenate([x_other, x_own], axis=0))
        hint_local = jnp.where(is_base, jnp.zeros((2 * tok_own, model_width), jnp.bfloat16), jnp.concatenate([hint_recv, hint_own], axis=0))
        start = (x_local.astype(jnp.float32) + mat_f32(hint_local, hint_proj)).astype(jnp.bfloat16)
        flat = lambda w: w.reshape(w.shape[:-3] + (model_width, model_width))
        hist = run_stack(start, in_norm[branch].astype(jnp.float32), in_qkv, flat(in_proj), in_up, in_down)
        ctrl_res = jnp.einsum("lnd,lde->lne", hist, zero_proj, preferred_element_type=jnp.float32).astype(jnp.bfloat16)
        res_recv = lax.ppermute(ctrl_res, "group", to_base)
        sums = (hist.astype(jnp.float32) + res_recv.astype(jnp.float32)).astype(jnp.bfloat16)
        out_state = run_stack(sums[layers], out_norm.astype(jnp.float32), out_qkv, flat(out_proj), out_up, out_down, skip_proj, sums[:layers][::-1])
        normed = layer_norm(out_state, final_norm[0], final_norm[1])
        y_local = mat_f32(normed, w_out).astype(jnp.bfloat16)
        y_recv = lax.ppermute(y_local[tok_own:], "group", to_ctrl)
        return jnp.where(is_base, y_local[:tok_own], y_recv)

    tok_spec = P(("data", "group"), None)
    return jax.shard_map(device_step, mesh=mesh, in_specs=(tok_spec, tok_spec) + (P(),) * 15, out_specs=tok_spec, check_vma=False)
```

time: 3030 us -> 450 us (0.15)
  waiting for transfers between devices: 2060 us -> 14.6 us
  Pallas kernels: 0 us -> 416 us
  local copies, waits for them, and re-layouts: 366 us -> 0.1 us
  matrix products: 297 us -> 3.43 us
  starting transfers between devices: 269 us -> 13.2 us
    ppermute x102 -> x0, waiting for transfers between devices: 2050 us -> none  [gather_half(): lax.ppermute(gathered, 'group', partner_perm)]
    pallas_call x0 -> x2, Pallas kernels: none -> 416 us  [run_stack(): pl.pallas_call(functools.partial(stack_kernel, n_blocks, two_branch, has_...]
    ppermute x102 -> x0, starting transfers between devices: 243 us -> none  [gather_half(): lax.ppermute(gathered, 'group', partner_perm)]
    slice x68 -> x1, local copies, waits for them, and re-layouts: 216 us -> 0.03 us  [device_step(): sums[:layers][::-1]]
    dot_general x61 -> x2, matrix products: 191 us -> 1.51 us  [mat_f32(): return jnp.dot(left_op, right_op, preferred_element_type=jnp.float32)]
    dot_general x34 -> x1, matrix products: 105 us -> 1.92 us  [device_step(): jnp.einsum('lnd,lde->lne', hist, zero_proj, preferred_element_type=jnp.fl...]
    unnamed x169 -> x12, local copies, waits for them, and re-layouts: 80.9 us -> 0.03 us
    concatenate x34 -> x0, local copies, waits for them, and re-layouts: 65.6 us -> none  [gather_half(): jnp.concatenate([gathered, lax.ppermute(gathered, 'group', partner_perm)]...]
  transfers between devices with their start and end apart: 114 -> 4, of which waited for: 105 -> 3; matrix products, arithmetic and copies ran while one was open for 10% -> 0% of each run, Pallas kernels for 0% -> 0%
where the time goes in v1:
time: 450 us
  Pallas kernels  416 us (92%)
  waiting for transfers between devices  14.6 us (3%)
  starting transfers between devices  13.2 us (3%)
    pallas_call x2, Pallas kernels, run_stack(): pl.pallas_call(functools.partial(stack_kernel, n_blocks, two_branch, has_...  416 us
    ppermute x1, waiting for transfers between devices, device_step(): res_recv = lax.ppermute(ctrl_res, 'group', to_base)  13.6 us
  transfers between devices with their start and end apart: 4, of which 3 were waited for; matrix products, arithmetic and copies ran while one was open for 0% of the time, Pallas kernels for 0%

profile of v1, /device:TPU:1, one launch (start us, length us, event | category | flops | bytes accessed | tf_op | source)
XLA Modules:
  0.0 449.9 jit_solution(11681630759125364445)
XLA Ops:
  0.0 0.0 copy-start
  0.0 4.4 collective-permute-start
  4.4 2.0 collective-permute-start.1
  6.5 0.8 bitcast_convert_fusion.refs_1_
  7.3 0.0 collective-permute-done
  7.3 0.1 collective-permute-done.1
  7.4 0.0 copy-done
  7.4 1.1 add_convert_fusion.1.refs_0_
  8.6 0.0 copy-start.2
  8.6 219.8 %in_stack.1 = bf16[9,32,768]{2,1,0:T(8,128)(2,1)S(1)} custom-call(bf16[32,768]{1,0:T(8,128)(2,1)S(1)} %add_convert_fusion.1.refs_0_, f32[9,4,768]{2,1,0:T(4,128)S(1)} %bitcast_convert_fusion.refs_1_, bf16[2,9,768,2304]{3,2,1,0:T(8,128)(2,1)} %refs_2_.1, bf16[2,9,768,768]{3,2,1,0:T(8,128)(2,1)} %bitcast.11, bf16[2,9,768,3072]{3,2,1,0:T(8,128)(2,1)} %refs_4_.2, ...), custom_call_target="tpu_custom_call" | custom-call | tf_op jit(solution)/shard_map/in_stack/pallas_call | solution.py:344
  228.4 0.0 copy-done.2
  228.4 0.0 copy-start.4
  228.4 0.0 copy-start.5
  228.4 1.9 convolution_convert_fusion
  230.3 1.3 collective-permute-start.2
  231.6 0.0 copy-done.4
  231.6 0.0 copy-done.5
  231.7 13.6 %collective-permute-done.2 = bf16[9,32,768]{2,1,0:T(8,128)(2,1)S(1)} collective-permute-done((bf16[9,32,768]{2,1,0:T(8,128)(2,1)S(1)}, bf16[9,32,768]{2,1,0:T(8,128)(2,1)S(1)}, u32[]{:S(2)}, u32[]{:S(2)}) %collective-permute-start.2) | collective-permute-done | bytes 442400 | tf_op jit(solution)/shard_map/ppermute | solution.py:372
  245.3 0.1 add_convert_fusion
  245.5 0.0 copy-start.3
  245.5 0.0 copy-start.1
  245.5 196.7 %out_stack.1 = bf16[32,768]{1,0:T(8,128)(2,1)S(1)} custom-call(bf16[32,768]{1,0:T(8,128)(2,1)S(1)} %slice_bitcast_fusion.refs_0_, bf16[8,32,768]{2,1,0:T(8,128)(2,1)S(1)} %rev.3.refs_1_, f32[8,4,768]{2,1,0:T(4,128)S(1)} %convert_element_type.47.refs_2_, bf16[8,1536,768]{2,1,0:T(8,128)(2,1)} %refs_3_.1, bf16[8,768,2304]{2,1,0:T(8,128)(2,1)} %refs_4_.3, ...), custom_call_target="tpu_custom_call" | custom-call | tf_op jit(solution)/shard_map/out_stack/pallas_call | solution.py:344
  442.2 0.1 convert_reduce_fusion
  442.3 0.2 fusion.2
  442.5 0.0 copy-done.3
  442.5 0.4 convolution_convert_fusion.1
  442.9 5.4 %collective-permute-start.3 = (bf16[16,768]{1,0:T(8,128)(2,1)S(1)}, bf16[16,768]{1,0:T(8,128)(2,1)S(1)}, u32[]{:S(2)}, u32[]{:S(2)}) collective-permute-start(bf16[16,768]{1,0:T(8,128)(2,1)S(1)} %slice.27), channel_id=1, source_target_pairs={{0,64},{1,65},{2,66},{3,67},{4,68},{5,69},{6,70},{7,71},{8,72},{9,... | collective-permute-start | bytes 73736 | tf_op jit(solution)/shard_map/ppermute | solution.py:377
  448.3 0.9 collective-permute-done.3
  449.2 0.6 slice_select_fusion
  449.9 0.0 copy-done.1
  (8 shorter events, 0.1 us)
Async XLA Ops:
  0.0 7.4 %copy-start = (bf16[768,768]{1,0:T(8,128)(2,1)S(1)}, bf16[768,768]{1,0:T(8,128)(2,1)}, u32[]{:S(2)}) copy-start(bf16[768,768]{1,0:T(8,128)(2,1)} %param.30) | copy-start | bytes 3538948
  0.0 7.3 %collective-permute-start = (bf16[16,768]{1,0:T(8,128)(2,1)}, bf16[16,768]{1,0:T(8,128)(2,1)S(1)}, u32[]{:S(2)}, u32[]{:S(2)}) collective-permute-start(bf16[16,768]{1,0:T(8,128)(2,1)} %param.17), channel_id=1, source_target_pairs={{0,64},{1,65},{2,66},{3,67},{4,68},{5,69},{6,70},{7,71},{8,72},{9,... | collective-permute-start | bytes 73736 | tf_op jit(solution)/shard_map/ppermute | solution.py:364
  4.4 3.0 collective-permute-start.1
  8.6 219.8 %copy-start.2 = (bf16[9,768,768]{2,1,0:T(8,128)(2,1)S(1)}, bf16[9,768,768]{2,1,0:T(8,128)(2,1)}, u32[]{:S(2)}) copy-start(bf16[9,768,768]{2,1,0:T(8,128)(2,1)} %param.29) | copy-start | bytes 31850500
  228.4 3.2 copy-start.4
  228.4 3.3 copy-start.5
  230.3 15.0 %collective-permute-start.2 = (bf16[9,32,768]{2,1,0:T(8,128)(2,1)S(1)}, bf16[9,32,768]{2,1,0:T(8,128)(2,1)S(1)}, u32[]{:S(2)}, u32[]{:S(2)}) collective-permute-start(bf16[9,32,768]{2,1,0:T(8,128)(2,1)S(1)} %convolution_convert_fusion), channel_id=1, source_target_pairs={{64,0},{65,1},{66,2},{67,3},{68,4},{69,5},{70,6},{71,7},{72,8},{73... | collective-permute-start | bytes 1327112 | tf_op jit(solution)/shard_map/ppermute | solution.py:372
  245.5 197.0 %copy-start.3 = (bf16[768,768]{1,0:T(8,128)(2,1)S(1)}, bf16[768,768]{1,0:T(8,128)(2,1)}, u32[]{:S(2)}) copy-start(bf16[768,768]{1,0:T(8,128)(2,1)} %param.33) | copy-start | bytes 3538948
  245.5 204.4 %copy-start.1 = (bf16[768,768]{1,0:T(8,128)(2,1)S(1)}, bf16[768,768]{1,0:T(8,128)(2,1)}, u32[]{:S(2)}) copy-start(bf16[768,768]{1,0:T(8,128)(2,1)} %param.30) | copy-start | bytes 3538948
  442.9 6.4 %collective-permute-start.3 = (bf16[16,768]{1,0:T(8,128)(2,1)S(1)}, bf16[16,768]{1,0:T(8,128)(2,1)S(1)}, u32[]{:S(2)}, u32[]{:S(2)}) collective-permute-start(bf16[16,768]{1,0:T(8,128)(2,1)S(1)} %slice.27), channel_id=1, source_target_pairs={{0,64},{1,65},{2,66},{3,67},{4,68},{5,69},{6,70},{7,71},{8,72},{9,... | collective-permute-start | bytes 73736 | tf_op jit(solution)/shard_map/ppermute | solution.py:377

commit v2 on v0

v2 whole, which is shorter than its diff:
```python
import functools

import jax
import jax.numpy as jnp
from jax import lax
from jax.experimental import pallas as pl
from jax.experimental.pallas import tpu as pltpu
from jax.sharding import PartitionSpec as P

EPS = 1e-6
MESH = pl.DeviceIdType.MESH
SCALE = 64 ** -0.5 * 1.4426950408889634
ROWS = 32
SLAB = 16


def mat_f32(left_op, right_op):
    return jnp.dot(left_op, right_op, preferred_element_type=jnp.float32)


def layer_norm(values, gain, shift):
    wide_vals = values.astype(jnp.float32)
    centered = wide_vals - jnp.mean(wide_vals, axis=-1, keepdims=True)
    variance = jnp.mean(centered * centered, axis=-1, keepdims=True)
    normed = centered * lax.rsqrt(variance + EPS)
    return (normed * gain + shift).astype(jnp.bfloat16)


def gelu(v):
    inner = 0.7978845608028654 * (v + 0.044715 * (v * v * v))
    return 0.5 * v * (1.0 + jnp.tanh(inner))


def net_kernel(x_ref, hint_ref, in_norm, out_norm, final_norm, in_qkv, in_proj, in_up, in_down,
               out_qkv, out_proj, out_up, out_down, zero_hbm, hint_hbm, skip_hbm, wout_hbm, y_ref,
               t_all, w_qkv, w_proj, w_up, w_down, w_skip, w_sq, v_buf, s_buf, top_buf, sum_buf, a_buf, a_full,
               u_buf, xh_buf, hist, r_out, r_in, y_out, y_in,
               w_sem, p1, p2, s1, q1, q2, f1, a_recv, a_send, x_recv, x_send, r_recv, r_send, y_recv, y_send):
    n_in, n_out = in_norm.shape[1], out_norm.shape[0]
    width = x_ref.shape[-1]
    half_w = width // 2
    hid = w_up.shape[-1]

    data_idx = lax.axis_index("data")
    me = lax.axis_index("group")
    core = lax.rem(me, 2)
    chip = me // 2
    x_pos = lax.rem(chip, 4)
    y_pos = lax.rem(chip // 4, 4)
    z_full = chip // 16
    half = z_full // 2
    z_pos = lax.rem(z_full, 2)
    sib_core = 1 - core
    sibling = me + 1 - 2 * core
    partner = me + 64 - 128 * half
    r_pos = y_pos + core * (x_pos - y_pos)
    d_pos = x_pos + core * (y_pos - x_pos)

    def dev(zz, r, d):
        yy = r + core * (d - r)
        xx = d + core * (r - d)
        return (((half * 2 + zz) * 4 + yy) * 4 + xx) * 2 + core

    def shift(pos, d):
        return lax.rem(pos + d + 4, 4)

    def z_of(dz):
        return z_pos if dz == 0 else 1 - z_pos

    def send(src, dst, target, send_sem, recv_sem):
        return pltpu.make_async_remote_copy(
            src_ref=src, dst_ref=dst, send_sem=send_sem, recv_sem=recv_sem,
            device_id=(data_idx, target), device_id_type=MESH)

    def remote(region, target, send_sem, recv_sem):
        return send(region, region, target, send_sem, recv_sem)

    def leg1(par, dz, d, receive=False):
        sems = (q1.at[dz, d], p1.at[par, dz, d])
        if receive:
            return remote(t_all.at[par, core, z_of(dz), r_pos, shift(d_pos, -d)], sibling, *sems)
        return remote(t_all.at[par, core, z_pos, r_pos, d_pos], dev(z_of(dz), r_pos, shift(d_pos, d)), *sems)

    def onward(dz, d):
        return (dz + (d in (1, 2))) % 2

    def leg2(par, dz, d, way, receive=False):
        sems = (q2.at[dz, d, way], p2.at[par, dz, d, way])
        zz, dd = z_of(dz), shift(d_pos, -d)
        if way < 2:
            w = 1 - 2 * way
            at, to = (shift(r_pos, -w) if receive else r_pos), shift(r_pos, w)
        elif (dz, d) == (1, 2):
            at, to = (shift(r_pos, 2) if receive else r_pos), shift(r_pos, 2)
        else:
            w = 1 - 2 * onward(dz, d)
            at, to = shift(r_pos, 2 if receive else -w), shift(r_pos, w)
        return remote(t_all.at[par, core, zz, at, dd], dev(z_pos, to, d_pos), *sems)

    def side(par, dz, ro, cc):
        at = shift(r_pos if cc is core else d_pos, ro)
        return remote(t_all.at[par, cc, z_of(dz), at], sibling, f1.at[dz, ro], s1.at[par, dz, ro])

    near = [(0, 1), (0, 3), (1, 0), (0, 2)]
    far = [(1, 1), (1, 3), (1, 2)]
    pieces = [(0, 0)] + near + far

    def local(src, dst, n):
        return pltpu.make_async_copy(src, dst, w_sem.at[n])

    def qkv_copies(ref, at):
        cols = lambda part: pl.ds(pl.multiple_of(part * width + core * half_w, 128), half_w)
        return [local(ref.at[(*at, slice(None), cols(p))], w_qkv.at[:, pl.ds(p * half_w, half_w)], p) for p in range(3)]

    def proj_copies(ref, at):
        return [local(ref.at[at], w_proj, 3)]

    def up_copies(ref, at):
        return [local(ref.at[at], w_up, 4)]

    def down_copies(ref, at):
        return [local(ref.at[at], w_down, 5)]

    def skip_copies(j):
        return [local(skip_hbm.at[j], w_skip, 6)]

    def square(ref):
        return [local(ref, w_sq, 7)]

    def start(copies):
        for c in copies:
            c.start()

    def wait(copies):
        for c in copies:
            c.wait()

    kinds = (qkv_copies, proj_copies, up_copies, down_copies)
    in_refs, out_refs = (in_qkv, in_proj, in_up, in_down), (out_qkv, out_proj, out_up, out_down)
    lane = lax.broadcasted_iota(jnp.int32, (2 * ROWS, 128), 1)

    def block(par, norm, copies, start_next, beside):
        t_all[par, core, z_pos, r_pos, d_pos] = layer_norm(u_buf[...], norm[0:1, :], norm[1:2, :])
        for key in near:
            leg1(par, *key).start()
        for way in (0, 1):
            leg2(par, 0, 0, way).start()
        for key in far:
            leg1(par, *key).start()
        beside(0)
        for key in near + far:
            leg1(par, *key, receive=True).wait_recv()
            for way in ((2, 0, 1) if key == (1, 2) else (0, 1)):
                leg2(par, *key, way).start()
        for dz in (0, 1):
            side(par, dz, 0, core).start()
        beside(1)

        seen = {}

        def take(dz, d, way):
            leg2(par, dz, d, way, receive=True).wait_recv()
            if way == onward(dz, d) and (dz, d) != (1, 2):
                leg2(par, dz, d, 2).start()
            seen[dz, way] = seen.get((dz, way), 0) + 1
            if seen[dz, way] == 4:
                side(par, dz, (3, 1, 2)[way], core).start()

        def take_both(keys):
            for key in keys:
                take(*key, onward(*key))
                take(*key, 1 - onward(*key))

        def chunk(j, cc, ro):
            at = shift(r_pos if cc is core else d_pos, ro)
            toks = jnp.concatenate([t_all[par, cc, zz, at, o] for zz in range(2) for o in range(4)], axis=0)
            n = toks.shape[0]
            kv = mat_f32(toks, w_qkv[:, half_w:3 * half_w]).astype(jnp.bfloat16)
            v_buf[j * n:(j + 1) * n, :] = kv[:, half_w:]
            for p in range(3):
                sc = lax.dot_general(q_bd[p], kv[:, p * 128:(p + 1) * 128], (((1,), (1,)), ((), ())), preferred_element_type=jnp.float32)
                top = jnp.max(sc, axis=-1, keepdims=True)
                if j:
                    old = top_buf[p, j - 1]
                    top = jnp.maximum(old, top)
                e = jnp.exp2((sc - top) * SCALE)
                s_buf[p, :, j * n:(j + 1) * n] = e
                part = e[:, 0:128] + e[:, 128:256]
                sum_buf[p] = sum_buf[p] * jnp.exp2((old - top) * SCALE) + part if j else part
                top_buf[p, j] = top

        take_both(pieces[0:4])
        wait(copies(0))
        for dz in (0, 1):
            side(par, dz, 0, sib_core).wait_recv()
        own = jnp.concatenate([t_all[par, 0, z_pos, y_pos, x_pos], t_all[par, 1, z_pos, x_pos, y_pos]], axis=0)
        q = mat_f32(own, w_qkv[:, 0:half_w])
        q_bd = []
        for p in range(3):
            qp = q[:, p * 128:(p + 1) * 128]
            q_bd.append(jnp.concatenate([jnp.where(lane < 64, qp, 0.0), jnp.where(lane < 64, 0.0, qp)], axis=0).astype(jnp.bfloat16))
        chunk(0, core, 0)
        take_both(pieces[4:6])
        chunk(1, sib_core, 0)
        take_both(pieces[6:8])
        chunk(2, core, 3)
        chunk(3, core, 1)
        for key in pieces:
            take(*key, 2)
        for j, ro in ((4, 3), (5, 1)):
            for dz in (0, 1):
                side(par, dz, ro, sib_core).wait_recv()
            chunk(j, sib_core, ro)
        chunk(6, core, 2)
        for dz in (0, 1):
            side(par, dz, 2, sib_core).wait_recv()
        chunk(7, sib_core, 2)
        start_next(0)

        n_chunks, n = 8, 256
        for p in range(3):
            top = top_buf[p, n_chunks - 1]
            inv = 1.0 / jnp.sum(sum_buf[p], axis=-1, keepdims=True)
            acc = None
            for j in range(n_chunks):
                fac = inv if j == n_chunks - 1 else jnp.exp2((top_buf[p, j] - top) * SCALE) * inv
                pr = (s_buf[p, :, j * n:(j + 1) * n] * fac).astype(jnp.bfloat16)
                o = mat_f32(pr, v_buf[j * n:(j + 1) * n, p * 128:(p + 1) * 128])
                acc = o if acc is None else acc + o
            a = jnp.where(lane < 64, acc[0:2 * ROWS], acc[2 * ROWS:4 * ROWS]).astype(jnp.bfloat16)
            a_buf[0, :, p * 128:(p + 1) * 128] = a[0:ROWS]
            a_buf[1, :, p * 128:(p + 1) * 128] = a[ROWS:2 * ROWS]

        swap = send(a_buf.at[sib_core], a_full.at[core], sibling, a_send, a_recv)
        swap.start()
        a_full[core] = a_buf[core]
        swap.wait_send()
        send(a_buf.at[core], a_full.at[sib_core], sibling, a_send, a_recv).wait_recv()

        wait(copies(1))
        attn = mat_f32(a_full[0], w_proj[0:half_w, :]) + mat_f32(a_full[1], w_proj[half_w:width, :])
        start_next(1)
        mid = (u_buf[...].astype(jnp.float32) + attn).astype(jnp.bfloat16)
        t2 = layer_norm(mid, norm[2:3, :], norm[3:4, :])
        wait(copies(2))
        wait(copies(3))
        acc = None
        for c in range(0, hid, width):
            h = gelu(mat_f32(t2, w_up[:, c:c + width])).astype(jnp.bfloat16)
            o = mat_f32(h, w_down[c:c + width, :])
            acc = o if acc is None else acc + o
        start_next(2)
        start_next(3)
        u_buf[...] = (mid.astype(jnp.float32) + acc).astype(jnp.bfloat16)

        for dz in (0, 1):
            for d in range(4):
                if dz or d:
                    leg1(par, dz, d).wait_send()
                for way in range(3):
                    leg2(par, dz, d, way).wait_send()
            for ro in range(4):
                side(par, dz, ro, core).wait_send()

    start(square(hint_hbm))
    for make, ref in zip(kinds, in_refs):
        start(make(ref, (half, 0)))
    start(skip_copies(0))

    def swap_in(n, src):
        return send(src, xh_buf.at[n, half], partner, x_send.at[n], x_recv.at[n])

    for n, ref in enumerate((x_ref, hint_ref)):
        swap_in(n, ref).start()
        xh_buf[n, half] = ref[...]
    for n, ref in enumerate((x_ref, hint_ref)):
        swap_in(n, ref).wait_send()
        send(ref, xh_buf.at[n, 1 - half], partner, x_send.at[n], x_recv.at[n]).wait_recv()

    @pl.when(half == 1)
    def _():
        r_in[...] = jnp.zeros_like(r_in)

    x_loc = jnp.concatenate([xh_buf[0, 0], xh_buf[0, 1]], axis=0)
    hint_loc = jnp.concatenate([xh_buf[1, 0], xh_buf[1, 1]], axis=0)
    wait(square(hint_hbm))
    hinted = (x_loc.astype(jnp.float32) + mat_f32(hint_loc, w_sq[...])).astype(jnp.bfloat16)
    start(square(zero_hbm.at[0]))
    u_buf[...] = x_loc

    @pl.when(half == 1)
    def _():
        u_buf[...] = hinted

    def residual(i):
        wait(square(zero_hbm.at[i]))
        r_out[...] = mat_f32(u_buf[...], w_sq[...]).astype(jnp.bfloat16)

    def residual_copy(i):
        return send(r_out, r_in.at[i], partner, r_send, r_recv.at[i])

    def in_block(i, carry):
        copies = lambda n: kinds[n](in_refs[n], (half, i))

        def start_next(n):
            @pl.when(i + 1 < n_in)
            def _():
                start(kinds[n](in_refs[n], (half, i + 1)))

            @pl.when(i + 1 == n_in)
            def _():
                start(kinds[n](out_refs[n], (0,)))

        def beside(when):
            @pl.when(i > 0)
            def _():
                if when == 0:
                    residual(i - 1)
                    start(square(zero_hbm.at[i]))
                else:
                    @pl.when(half == 1)
                    def _():
                        residual_copy(i - 1).start()

        block(lax.rem(i, 2), in_norm.at[half, i], copies, start_next, beside)
        hist[i] = u_buf[...]

        @pl.when(jnp.logical_and(i > 0, half == 1))
        def _():
            residual_copy(i - 1).wait_send()

        return carry

    lax.fori_loop(0, n_in, in_block, 0)
    residual(n_in - 1)
    start(square(wout_hbm))

    @pl.when(half == 1)
    def _():
        residual_copy(n_in - 1).start()
        residual_copy(n_in - 1).wait_send()

    @pl.when(half == 0)
    def _():
        for i in range(n_in):
            residual_copy(i).wait_recv()

    def with_residual(i):
        return (hist[i].astype(jnp.float32) + r_in[i].astype(jnp.float32)).astype(jnp.bfloat16)

    u_buf[...] = with_residual(n_in - 1)

    def out_block(j, carry):
        copies = lambda n: kinds[n](out_refs[n], (j,))

        def start_next(n):
            @pl.when(j + 1 < n_out)
            def _():
                start(kinds[n](out_refs[n], (j + 1,)))

        wait(skip_copies(j))
        merged = mat_f32(u_buf[...], w_skip[0:width, :]) + mat_f32(with_residual(n_out - 1 - j), w_skip[width:2 * width, :])

        @pl.when(j + 1 < n_out)
        def _():
            start(skip_copies(j + 1))

        u_buf[...] = merged.astype(jnp.bfloat16)
        block(lax.rem(j + n_in, 2), out_norm.at[j], copies, start_next, lambda when: None)
        return carry

    lax.fori_loop(0, n_out, out_block, 0)

    normed = layer_norm(u_buf[...], final_norm[0:1, :], final_norm[1:2, :])
    wait(square(wout_hbm))
    y = mat_f32(normed, w_sq[...]).astype(jnp.bfloat16)
    y_out[0] = y[0:SLAB]
    y_out[1] = y[SLAB:ROWS]
    hand_over = send(y_out.at[1], y_in, partner, y_send, y_recv)

    @pl.when(half == 0)
    def _():
        hand_over.start()
        y_ref[...] = y_out[0]
        hand_over.wait_send()

    @pl.when(half == 1)
    def _():
        hand_over.wait_recv()
        y_ref[...] = y_in[...]


def solution(mesh):
    def device_step(x_own, hint_own, in_qkv, in_proj, in_up, in_down, in_norm, out_qkv, out_proj, out_up, out_down, out_norm, zero_proj, hint_proj, skip_proj, final_norm, w_out):
        width, hid, n_in = x_own.shape[-1], in_up.shape[-1], zero_proj.shape[0]
        vmem, hbm = pl.BlockSpec(memory_space=pltpu.VMEM), pl.BlockSpec(memory_space=pl.ANY)
        bf, f32, dma = jnp.bfloat16, jnp.float32, pltpu.SemaphoreType.DMA
        flat = lambda w: w.reshape(w.shape[:-3] + (width, width))
        scratch = [
            pltpu.VMEM((2, 2, 2, 4, 4, ROWS, width), bf),
            pltpu.VMEM((width, 3 * width // 2), bf), pltpu.VMEM((width, width), bf),
            pltpu.VMEM((width, hid), bf), pltpu.VMEM((hid, width), bf),
            pltpu.VMEM((2 * width, width), bf), pltpu.VMEM((width, width), bf),
            pltpu.VMEM((2048, width // 2), bf), pltpu.VMEM((3, 128, 2048), f32),
            pltpu.VMEM((3, 8, 128, 1), f32), pltpu.VMEM((3, 128, 128), f32),
            pltpu.VMEM((2, ROWS, width // 2), bf), pltpu.VMEM((2, ROWS, width // 2), bf),
            pltpu.VMEM((ROWS, width), bf), pltpu.VMEM((2, 2, SLAB, width), bf),
            pltpu.VMEM((n_in, ROWS, width), bf), pltpu.VMEM((ROWS, width), bf), pltpu.VMEM((n_in, ROWS, width), bf),
            pltpu.VMEM((2, SLAB, width), bf), pltpu.VMEM((SLAB, width), bf),
            dma((8,)),
            dma((2, 2, 4)), dma((2, 2, 4, 3)), dma((2, 2, 4)), dma((2, 4)), dma((2, 4, 3)), dma((2, 4)),
            dma(()), dma(()), dma((2,)), dma((2,)), dma((n_in,)), dma(()), dma(()), dma(()),
        ]
        return pl.pallas_call(
            net_kernel,
            out_shape=jax.ShapeDtypeStruct(x_own.shape, bf), in_specs=[vmem] * 5 + [hbm] * 12, out_specs=vmem,
            scratch_shapes=scratch, name="net",
            compiler_params=pltpu.CompilerParams(has_side_effects=True, vmem_limit_bytes=52 * 1024 * 1024),
        )(x_own, hint_own, in_norm.astype(f32), out_norm.astype(f32), final_norm.astype(f32), in_qkv, flat(in_proj), in_up, in_down,
          out_qkv, flat(out_proj), out_up, out_down, zero_proj, hint_proj, skip_proj, w_out)

    tok_spec = P(("data", "group"), None)
    return jax.shard_map(device_step, mesh=mesh, in_specs=(tok_spec, tok_spec) + (P(),) * 15, out_specs=tok_spec, check_vma=False)
```

time: 3030 us -> 424 us (0.14)
  waiting for transfers between devices: 2060 us -> 0 us
  Pallas kernels: 0 us -> 418 us
  local copies, waits for them, and re-layouts: 366 us -> 3.35 us
  matrix products: 297 us -> 0 us
  starting transfers between devices: 269 us -> 0 us
    ppermute x114 -> x0, waiting for transfers between devices: 2060 us -> none  [the longest x102 2050 us: gather_half(): lax.ppermute(gathered, 'group', partner_perm)]
    pallas_call x0 -> x1, Pallas kernels: none -> 418 us  [device_step(): pl.pallas_call(net_kernel, out_shape=jax.ShapeDtypeStruct(x_own.shape, bf...]
    dot_general x95 -> x0, matrix products: 297 us -> none  [the longest x61 191 us: mat_f32(): return jnp.dot(left_op, right_op, preferred_element_type=jnp.float32)]
    ppermute x114 -> x0, starting transfers between devices: 269 us -> none  [the longest x102 243 us: gather_half(): lax.ppermute(gathered, 'group', partner_perm)]
    slice x69 -> x0, local copies, waits for them, and re-layouts: 216 us -> none  [the longest x34 134 us: transformer_block(): key_heads = key_vals[:, :model_width].reshape(-1, head_count, head_dim)]
    unnamed x169 -> x7, local copies, waits for them, and re-layouts: 80.9 us -> 3.35 us
    concatenate x34 -> x0, local copies, waits for them, and re-layouts: 65.6 us -> none  [gather_half(): jnp.concatenate([gathered, lax.ppermute(gathered, 'group', partner_perm)]...]
  transfers between devices with their start and end apart: 114 -> 0, of which waited for: 105 -> 0; matrix products, arithmetic and copies ran while one was open for 10% -> 0% of each run, Pallas kernels for 0% -> 0%
where the time goes in v2:
time: 424 us
  Pallas kernels  418 us (99%)
    pallas_call x1, Pallas kernels, device_step(): pl.pallas_call(net_kernel, out_shape=jax.ShapeDtypeStruct(x_own.shape, bf...  418 us

profile of v2, /device:TPU:1, one launch (start us, length us, event | category | flops | bytes accessed | tf_op | source)
XLA Modules:
  0.0 423.7 jit_solution(12843562031698990647)
XLA Ops:
  0.0 0.7 convert_element_type.11.final_norm
  0.7 0.8 convert_element_type.10.out_norm
  1.5 0.9 convert_element_type.9.in_norm
  2.4 0.0 copy-start
  2.4 1.3 copy-done
  3.7 0.0 copy-start.1
  3.7 0.7 copy-done.1
  4.4 0.0 copy-start.2
  4.4 0.7 copy-done.2
  5.2 417.9 %net.1 = bf16[16,768]{1,0:T(8,128)(2,1)S(1)} custom-call(bf16[16,768]{1,0:T(8,128)(2,1)S(1)} %copy-done.1, bf16[16,768]{1,0:T(8,128)(2,1)S(1)} %copy-done.2, f32[2,9,4,768]{3,2,1,0:T(4,128)S(1)} %convert_element_type.9.in_norm, f32[8,4,768]{2,1,0:T(4,128)S(1)} %convert_element_type.10.out_norm, f32[2,768]{1,0:T(2,128)S(1)} %convert_element_type.11.final_norm, ...), custom_call_target="tpu_custom_call" | custom-call | tf_op jit(solution)/shard_map/net/pallas_call | solution.py:414
  423.1 0.6 copy.19
Async XLA Ops:
  2.4 1.3 copy-start
  3.7 0.7 copy-start.1
  4.4 0.7 copy-start.2

commit v3 on v2

--- a/solution.py
+++ b/solution.py
@@ -33,7 +33,7 @@
 
 def net_kernel(x_ref, hint_ref, in_norm, out_norm, final_norm, in_qkv, in_proj, in_up, in_down,
                out_qkv, out_proj, out_up, out_down, zero_hbm, hint_hbm, skip_hbm, wout_hbm, y_ref,
-               t_all, w_qkv, w_proj, w_up, w_down, w_skip, w_sq, v_buf, s_buf, top_buf, sum_buf, a_buf, a_full,
+               t_all, w_qkv, w_proj, w_up, w_down, w_skip, w_sq, v_buf, s_buf, top_buf, a_buf, a_full,
                u_buf, xh_buf, hist, r_out, r_in, y_out, y_in,
                w_sem, p1, p2, s1, q1, q2, f1, a_recv, a_send, x_recv, x_send, r_recv, r_send, y_recv, y_send):
     n_in, n_out = in_norm.shape[1], out_norm.shape[0]
@@ -179,20 +179,17 @@
             v_buf[j * n:(j + 1) * n, :] = kv[:, half_w:]
             for p in range(3):
                 sc = lax.dot_general(q_bd[p], kv[:, p * 128:(p + 1) * 128], (((1,), (1,)), ((), ())), preferred_element_type=jnp.float32)
-                top = jnp.max(sc, axis=-1, keepdims=True)
-                if j:
-                    old = top_buf[p, j - 1]
-                    top = jnp.maximum(old, top)
-                e = jnp.exp2((sc - top) * SCALE)
-                s_buf[p, :, j * n:(j + 1) * n] = e
-                part = e[:, 0:128] + e[:, 128:256]
-                sum_buf[p] = sum_buf[p] * jnp.exp2((old - top) * SCALE) + part if j else part
-                top_buf[p, j] = top
-
-        take_both(pieces[0:4])
+                s_buf[p, :, j * n:(j + 1) * n] = sc
+                top = jnp.maximum(sc[:, 0:128], sc[:, 128:256])
+                top_buf[p] = jnp.maximum(top_buf[p], top) if j else top
+
+        def side_in(ro):
+            for dz in (0, 1):
+                side(par, dz, ro, sib_core).wait_recv()
+
+        take_both(pieces)
         wait(copies(0))
-        for dz in (0, 1):
-            side(par, dz, 0, sib_core).wait_recv()
+        side_in(0)
         own = jnp.concatenate([t_all[par, 0, z_pos, y_pos, x_pos], t_all[par, 1, z_pos, x_pos, y_pos]], axis=0)
         q = mat_f32(own, w_qkv[:, 0:half_w])
         q_bd = []
@@ -200,31 +197,33 @@
             qp = q[:, p * 128:(p + 1) * 128]
             q_bd.append(jnp.concatenate([jnp.where(lane < 64, qp, 0.0), jnp.where(lane < 64, 0.0, qp)], axis=0).astype(jnp.bfloat16))
         chunk(0, core, 0)
-        take_both(pieces[4:6])
         chunk(1, sib_core, 0)
-        take_both(pieces[6:8])
         chunk(2, core, 3)
         chunk(3, core, 1)
         for key in pieces:
             take(*key, 2)
-        for j, ro in ((4, 3), (5, 1)):
-            for dz in (0, 1):
-                side(par, dz, ro, sib_core).wait_recv()
-            chunk(j, sib_core, ro)
+        side_in(3)
+        chunk(4, sib_core, 3)
+        side_in(1)
+        chunk(5, sib_core, 1)
         chunk(6, core, 2)
-        for dz in (0, 1):
-            side(par, dz, 2, sib_core).wait_recv()
+        side_in(2)
         chunk(7, sib_core, 2)
         start_next(0)
 
         n_chunks, n = 8, 256
         for p in range(3):
-            top = top_buf[p, n_chunks - 1]
-            inv = 1.0 / jnp.sum(sum_buf[p], axis=-1, keepdims=True)
+            top = jnp.max(top_buf[p], axis=-1, keepdims=True)
+            part = None
+            for j in range(n_chunks):
+                e = jnp.exp2((s_buf[p, :, j * n:(j + 1) * n] - top) * SCALE)
+                s_buf[p, :, j * n:(j + 1) * n] = e
+                both = e[:, 0:128] + e[:, 128:256]
+                part = both if part is None else part + both
+            inv = 1.0 / jnp.sum(part, axis=-1, keepdims=True)
             acc = None
             for j in range(n_chunks):
-                fac = inv if j == n_chunks - 1 else jnp.exp2((top_buf[p, j] - top) * SCALE) * inv
-                pr = (s_buf[p, :, j * n:(j + 1) * n] * fac).astype(jnp.bfloat16)
+                pr = (s_buf[p, :, j * n:(j + 1) * n] * inv).astype(jnp.bfloat16)
                 o = mat_f32(pr, v_buf[j * n:(j + 1) * n, p * 128:(p + 1) * 128])
                 acc = o if acc is None else acc + o
             a = jnp.where(lane < 64, acc[0:2 * ROWS], acc[2 * ROWS:4 * ROWS]).astype(jnp.bfloat16)
@@ -402,7 +401,7 @@
             pltpu.VMEM((width, hid), bf), pltpu.VMEM((hid, width), bf),
             pltpu.VMEM((2 * width, width), bf), pltpu.VMEM((width, width), bf),
             pltpu.VMEM((2048, width // 2), bf), pltpu.VMEM((3, 128, 2048), f32),
-            pltpu.VMEM((3, 8, 128, 1), f32), pltpu.VMEM((3, 128, 128), f32),
+            pltpu.VMEM((3, 128, 128), f32),
             pltpu.VMEM((2, ROWS, width // 2), bf), pltpu.VMEM((2, ROWS, width // 2), bf),
             pltpu.VMEM((ROWS, width), bf), pltpu.VMEM((2, 2, SLAB, width), bf),
             pltpu.VMEM((n_in, ROWS, width), bf), pltpu.VMEM((ROWS, width), bf), pltpu.VMEM((n_in, ROWS, width), bf),

time: 424 us -> 395 us (0.932)
  Pallas kernels: 418 us -> 389 us
    pallas_call x1, Pallas kernels: 418 us -> 389 us  [device_step(): pl.pallas_call(net_kernel, out_shape=jax.ShapeDtypeStruct(x_own.shape, bf...]
where the time goes in v3:
time: 395 us
  Pallas kernels  389 us (98%)
    pallas_call x1, Pallas kernels, device_step(): pl.pallas_call(net_kernel, out_shape=jax.ShapeDtypeStruct(x_own.shape, bf...  389 us

profile of v3, /device:TPU:1, one launch (start us, length us, event | category | flops | bytes accessed | tf_op | source)
XLA Modules:
  0.0 394.7 jit_solution(12802499034718787284)
XLA Ops:
  0.0 0.7 convert_element_type.11.final_norm
  0.7 0.8 convert_element_type.10.out_norm
  1.5 0.9 convert_element_type.9.in_norm
  2.4 0.0 copy-start
  2.4 1.3 copy-done
  3.7 0.0 copy-start.1
  3.7 0.7 copy-done.1
  4.4 0.0 copy-start.2
  4.4 0.7 copy-done.2
  5.2 389.0 %net.1 = bf16[16,768]{1,0:T(8,128)(2,1)S(1)} custom-call(bf16[16,768]{1,0:T(8,128)(2,1)S(1)} %copy-done.1, bf16[16,768]{1,0:T(8,128)(2,1)S(1)} %copy-done.2, f32[2,9,4,768]{3,2,1,0:T(4,128)S(1)} %convert_element_type.9.in_norm, f32[8,4,768]{2,1,0:T(4,128)S(1)} %convert_element_type.10.out_norm, f32[2,768]{1,0:T(2,128)S(1)} %convert_element_type.11.final_norm, ...), custom_call_target="tpu_custom_call" | custom-call | tf_op jit(solution)/shard_map/net/pallas_call | solution.py:413
  394.1 0.6 copy.19
Async XLA Ops:
  2.4 1.3 copy-start
  3.7 0.7 copy-start.1
  4.4 0.7 copy-start.2
